TPU v7x, 8 devices: a whole 2x2x1 slice. The times are simulated.
8 devices in a mesh: data: 1 (over z), ctxo: 2 (over y), ctx: 4 (over x, core).
Axes of the slice: x: 2, y: 2, z: 1, core: 2. Of those that a mesh axis runs over, the one named last changes fastest.
Arguments:
- q_seq: bfloat16 [16, 4096, 4, 128], P('data', ('ctxo', 'ctx'))
- k_seq: bfloat16 [16, 4096, 1, 128], P('data', ('ctxo', 'ctx'))
- v_seq: bfloat16 [16, 4096, 1, 128], P('data', ('ctxo', 'ctx'))
- do_seq: bfloat16 [16, 4096, 4, 128], P('data', ('ctxo', 'ctx'))
Outputs:
- output 1: bfloat16 [16, 4096, 4, 128], P('data', ('ctxo', 'ctx'))
- output 2: bfloat16 [16, 4096, 4, 128], P('data', ('ctxo', 'ctx'))
- output 3: bfloat16 [16, 4096, 1, 128], P('data', ('ctxo', 'ctx'))
- output 4: bfloat16 [16, 4096, 1, 128], P('data', ('ctxo', 'ctx'))
All inputs are finite; a program needn't handle non-finite values.
Results may differ from a plain program's by a relative error of at most 0.0124163.
Values are sent between devices in bfloat16 or wider.
A program may use at most 1 GiB of HBM per device.

v0:
```python
import math
import jax
import jax.numpy as jnp
from jax import lax
from jax.sharding import PartitionSpec as P

CTX_AXES = ('ctxo', 'ctx')


def causal_mask(n_rows):
    row_ids = lax.broadcasted_iota(jnp.int32, (n_rows, 1, n_rows), 0)
    col_ids = lax.broadcasted_iota(jnp.int32, (n_rows, 1, n_rows), 2)
    return row_ids >= col_ids


def pair_forward(q_blk, k_blk, v_blk, key_mask):
    q_scale = 1.0 / math.sqrt(q_blk.shape[-1])
    scores = jnp.einsum('bqhgd,bkhd->bhqgk', q_blk, k_blk, preferred_element_type=jnp.float32) * q_scale
    if key_mask is not None:
        scores = jnp.where(key_mask, scores, -jnp.inf)
    row_max = jnp.max(scores, axis=-1)
    prob_blk = jnp.exp(scores - row_max[..., None])
    row_sum = jnp.sum(prob_blk, axis=-1)
    out_blk = jnp.einsum('bhqgk,bkhd->bhqgd', prob_blk.astype(jnp.bfloat16), v_blk, preferred_element_type=jnp.float32)
    return out_blk / row_sum[..., None], row_max + jnp.log(row_sum)


def merge_parts(out_a, lse_a, out_b, lse_b):
    lse_new = jnp.logaddexp(lse_a, lse_b)
    out_new = out_a * jnp.exp(lse_a - lse_new)[..., None] + out_b * jnp.exp(lse_b - lse_new)[..., None]
    return out_new, lse_new


def pair_backward(q_blk, do_blk, lse_blk, drow_blk, k_blk, v_blk, key_mask):
    q_scale = 1.0 / math.sqrt(q_blk.shape[-1])
    scores = jnp.einsum('bqhgd,bkhd->bhqgk', q_blk, k_blk, preferred_element_type=jnp.float32) * q_scale
    if key_mask is not None:
        scores = jnp.where(key_mask, scores, -jnp.inf)
    prob_blk = jnp.exp(scores - lse_blk[..., None])
    dv_part = jnp.einsum('bhqgk,bqhgd->bhkd', prob_blk.astype(jnp.bfloat16), do_blk, preferred_element_type=jnp.float32)
    prob_grad = jnp.einsum('bqhgd,bkhd->bhqgk', do_blk, v_blk, preferred_element_type=jnp.float32)
    score_grad = (prob_blk * (prob_grad - drow_blk[..., None])).astype(jnp.bfloat16)
    dq_part = jnp.einsum('bhqgk,bkhd->bhqgd', score_grad, k_blk, preferred_element_type=jnp.float32) * q_scale
    dk_part = jnp.einsum('bhqgk,bqhgd->bhkd', score_grad, q_blk, preferred_element_type=jnp.float32) * q_scale
    return dq_part, dk_part, dv_part


def solution(mesh):
    n_ctx = mesh.shape['ctxo'] * mesh.shape['ctx']
    half_ctx = n_ctx // 2
    next_perm = [(src_idx, (src_idx + 1) % n_ctx) for src_idx in range(n_ctx)]
    home_kv = [(src_idx, (src_idx - half_ctx) % n_ctx) for src_idx in range(n_ctx)]
    home_q = [(src_idx, (src_idx - half_ctx + 1) % n_ctx) for src_idx in range(n_ctx)]
    blk_spec = P('data', CTX_AXES, None, None)

    def send_next(tree_in):
        return lax.ppermute(tree_in, CTX_AXES, next_perm)

    def local_attn(q_in, k_in, v_in, do_in):
        batch_rows, chunk_len, q_heads, head_dim = q_in.shape
        kv_heads = k_in.shape[2]
        row_shape = (batch_rows, chunk_len, kv_heads, q_heads // kv_heads, head_dim)
        rank_idx = lax.axis_index(CTX_AXES)
        q_own = q_in.reshape(row_shape)
        do_own = do_in.reshape(row_shape)
        diag_mask = causal_mask(chunk_len)
        last_owner = rank_idx >= half_ctx

        own_out, own_lse = pair_forward(q_own, k_in, v_in, diag_mask)

        def fwd_step(step_idx, state_in):
            own_out, own_lse, k_buf, v_buf, q_buf, hlp_out, hlp_lse = state_in
            k_buf, v_buf, q_buf, hlp_out, hlp_lse = send_next((k_buf, v_buf, q_buf, hlp_out, hlp_lse))
            is_owner = rank_idx >= step_idx
            part_out, part_lse = pair_forward(jnp.where(is_owner, q_own, q_buf), jnp.where(is_owner, k_buf, k_in), jnp.where(is_owner, v_buf, v_in), None)
            new_out, new_lse = merge_parts(jnp.where(is_owner, own_out, hlp_out), jnp.where(is_owner, own_lse, hlp_lse), part_out, part_lse)
            own_out = jnp.where(is_owner, new_out, own_out)
            own_lse = jnp.where(is_owner, new_lse, own_lse)
            hlp_out = jnp.where(is_owner, hlp_out, new_out)
            hlp_lse = jnp.where(is_owner, hlp_lse, new_lse)
            return own_out, own_lse, k_buf, v_buf, q_buf, hlp_out, hlp_lse

        fwd_state = (own_out, own_lse, k_in, v_in, q_own, jnp.zeros_like(own_out), jnp.full_like(own_lse, -jnp.inf))
        own_out, own_lse, k_buf, v_buf, q_buf, hlp_out, hlp_lse = lax.fori_loop(1, half_ctx, fwd_step, fwd_state)
        k_buf, v_buf = send_next((k_buf, v_buf))
        part_out, part_lse = pair_forward(q_own, k_buf, v_buf, None)
        new_out, new_lse = merge_parts(own_out, own_lse, part_out, part_lse)
        own_out = jnp.where(last_owner, new_out, own_out)
        own_lse = jnp.where(last_owner, new_lse, own_lse)
        hlp_out, hlp_lse = lax.ppermute((hlp_out, hlp_lse), CTX_AXES, home_q)
        own_out, own_lse = merge_parts(own_out, own_lse, hlp_out, hlp_lse)

        drow_own = jnp.sum(jnp.swapaxes(do_own, 1, 2) * own_out, axis=-1)
        dq_own, dk_own, dv_own = pair_backward(q_own, do_own, own_lse, drow_own, k_in, v_in, diag_mask)

        def bwd_step(step_idx, state_in):
            dq_own, dk_own, dv_own, kv_bundle, q_bundle = state_in
            kv_bundle, q_bundle = send_next((kv_bundle, q_bundle))
            k_buf, v_buf, dk_buf, dv_buf = kv_bundle
            q_buf, do_buf, lse_buf, drow_buf, dq_buf = q_bundle
            is_owner = rank_idx >= step_idx
            dq_part, dk_part, dv_part = pair_backward(
                jnp.where(is_owner, q_own, q_buf), jnp.where(is_owner, do_own, do_buf),
                jnp.where(is_owner, own_lse, lse_buf), jnp.where(is_owner, drow_own, drow_buf),
                jnp.where(is_owner, k_buf, k_in), jnp.where(is_owner, v_buf, v_in), None)
            dq_own = jnp.where(is_owner, dq_own + dq_part, dq_own)
            dk_own = jnp.where(is_owner, dk_own, dk_own + dk_part)
            dv_own = jnp.where(is_owner, dv_own, dv_own + dv_part)
            kv_bundle = (k_buf, v_buf, jnp.where(is_owner, dk_buf + dk_part, dk_buf), jnp.where(is_owner, dv_buf + dv_part, dv_buf))
            q_bundle = (q_buf, do_buf, lse_buf, drow_buf, jnp.where(is_owner, dq_buf, dq_buf + dq_part))
            return dq_own, dk_own, dv_own, kv_bundle, q_bundle

        kv_bundle = (k_in, v_in, jnp.zeros_like(dk_own), jnp.zeros_like(dv_own))
        q_bundle = (q_own, do_own, own_lse, drow_own, jnp.zeros_like(dq_own))
        dq_own, dk_own, dv_own, kv_bundle, q_bundle = lax.fori_loop(1, half_ctx, bwd_step, (dq_own, dk_own, dv_own, kv_bundle, q_bundle))
        k_buf, v_buf, dk_buf, dv_buf = send_next(kv_bundle)
        dq_part, dk_part, dv_part = pair_backward(q_own, do_own, own_lse, drow_own, k_buf, v_buf, None)
        dq_own = jnp.where(last_owner, dq_own + dq_part, dq_own)
        dk_buf = jnp.where(last_owner, dk_buf + dk_part, dk_buf)
        dv_buf = jnp.where(last_owner, dv_buf + dv_part, dv_buf)
        dk_buf, dv_buf = lax.ppermute((dk_buf, dv_buf), CTX_AXES, home_kv)
        dq_buf = lax.ppermute(q_bundle[4], CTX_AXES, home_q)
        out_seq = jnp.swapaxes(own_out.astype(jnp.bfloat16), 1, 2).reshape(q_in.shape)
        dq_seq = jnp.swapaxes((dq_own + dq_buf).astype(jnp.bfloat16), 1, 2).reshape(q_in.shape)
        dk_seq = jnp.swapaxes((dk_own + dk_buf).astype(jnp.bfloat16), 1, 2)
        dv_seq = jnp.swapaxes((dv_own + dv_buf).astype(jnp.bfloat16), 1, 2)
        return out_seq, dq_seq, dk_seq, dv_seq

    return jax.shard_map(local_attn, mesh=mesh, in_specs=(blk_spec, blk_spec, blk_spec, blk_spec), out_specs=(blk_spec, blk_spec, blk_spec, blk_spec), check_vma=False)
```

profile of v0, /device:TPU:2, one launch (start us, length us, event | category | flops | bytes accessed | tf_op | source)
XLA Modules:
  0.0 4291.2 jit_solution(14479496506695388766)
XLA Ops:
  59.2 33.2 divide_bitcast_fusion
  103.0 1300.5 %while.62 = (s32[]{:T(128)}, f32[16,1,512,4,128]{4,2,3,0,1:T(8,128)}, f32[16,1,512,4]{2,3,0,1:T(4,128)S(1)}, bf16[16,512,1,128]{3,1,0,2:T(8,128)(2,1)}, bf16[16,...) while((s32[]{:T(128)}, ...), condition=%wide.region_5.6_spmd.clone, body=%wide.region_2.5_spmd.clone.sunk | while | flops 8764489728 | bytes 481689984 | solution.py:84
  112.7 291.8 %collective-permute-done.2 = bf16[16,512,1,128]{3,1,0,2:T(8,128)(2,1)} collective-permute-done((bf16[16,512,1,128]{3,1,0,2:T(8,128)(2,1)}, bf16[16,512,1,128]{3,1,0,2:T(8,128)(2,1)}, u32[]{:S(2)}, u32[]{:S(2)}) %collective-permute-start.2) | collective-permute-done | bytes 2097184 | tf_op jit(solution)/shard_map/while/body/eval_jaxpr/ppermute | solution.py:57
  486.4 47.0 %broadcast_select_fusion.32 = (f32[16,1,512,4,128]{4,2,3,0,1:T(8,128)}, f32[16,1,512,4,128]{4,2,3,0,1:T(8,128)}) fusion(f32[16,1,512,4,128]{4,2,3,0,1:T(8,128)} %collective-permute-done, pred[]{:T(512)S(6)} %ge.30, f32[16,1,512,4,128]{4,2,3,0,1:T(8,128)} %get-tuple-element.1016, f32[16,512,4]{1,2,0:T(4,128)S(1)} %get-tuple-element.969, ...), kind=kOutput, calls=%fused_computation.13.clone.3 | convolution fusion | flops 4375707648 | bytes 138936320 | tf_op jit(solution)/shard_map/while/body/eval_jaxpr/bhqgk,bkhd->bhqgd/dot_general | solution.py:24
  548.2 291.8 %collective-permute-done.2 = bf16[16,512,1,128]{3,1,0,2:T(8,128)(2,1)} collective-permute-done((bf16[16,512,1,128]{3,1,0,2:T(8,128)(2,1)}, bf16[16,512,1,128]{3,1,0,2:T(8,128)(2,1)}, u32[]{:S(2)}, u32[]{:S(2)}) %collective-permute-start.2) | collective-permute-done | bytes 2097184 | tf_op jit(solution)/shard_map/while/body/eval_jaxpr/ppermute | solution.py:57
  922.0 47.0 %broadcast_select_fusion.32 = (f32[16,1,512,4,128]{4,2,3,0,1:T(8,128)}, f32[16,1,512,4,128]{4,2,3,0,1:T(8,128)}) fusion(f32[16,1,512,4,128]{4,2,3,0,1:T(8,128)} %collective-permute-done, pred[]{:T(512)S(6)} %ge.30, f32[16,1,512,4,128]{4,2,3,0,1:T(8,128)} %get-tuple-element.1016, f32[16,512,4]{1,2,0:T(4,128)S(1)} %get-tuple-element.969, ...), kind=kOutput, calls=%fused_computation.13.clone.3 | convolution fusion | flops 4375707648 | bytes 138936320 | tf_op jit(solution)/shard_map/while/body/eval_jaxpr/bhqgk,bkhd->bhqgd/dot_general | solution.py:24
  984.0 291.6 %collective-permute-done.2 = bf16[16,512,1,128]{3,1,0,2:T(8,128)(2,1)} collective-permute-done((bf16[16,512,1,128]{3,1,0,2:T(8,128)(2,1)}, bf16[16,512,1,128]{3,1,0,2:T(8,128)(2,1)}, u32[]{:S(2)}, u32[]{:S(2)}) %collective-permute-start.2) | collective-permute-done | bytes 2097184 | tf_op jit(solution)/shard_map/while/body/eval_jaxpr/ppermute | solution.py:57
  1356.9 46.6 %broadcast_select_fusion.32 = (f32[16,1,512,4,128]{4,2,3,0,1:T(8,128)}, f32[16,1,512,4,128]{4,2,3,0,1:T(8,128)}) fusion(f32[16,1,512,4,128]{4,2,3,0,1:T(8,128)} %collective-permute-done, pred[]{:T(512)S(6)} %ge.30, f32[16,1,512,4,128]{4,2,3,0,1:T(8,128)} %get-tuple-element.1016, f32[16,512,4]{1,2,0:T(4,128)S(1)} %get-tuple-element.969, ...), kind=kOutput, calls=%fused_computation.13.clone.3 | convolution fusion | flops 4375707648 | bytes 138936320 | tf_op jit(solution)/shard_map/while/body/eval_jaxpr/bhqgk,bkhd->bhqgd/dot_general | solution.py:24
  1489.1 139.9 %collective-permute-done.14 = bf16[16,512,1,128]{3,1,0,2:T(8,128)(2,1)} collective-permute-done((bf16[16,512,1,128]{3,1,0,2:T(8,128)(2,1)}, bf16[16,512,1,128]{3,1,0,2:T(8,128)(2,1)}, u32[]{:S(2)}, u32[]{:S(2)}) %collective-permute-start.14) | collective-permute-done | bytes 2097184 | tf_op jit(solution)/shard_map/ppermute | solution.py:57
  1677.1 107.5 %collective-permute-done.16 = f32[16,1,512,4]{2,3,0,1:T(4,128)S(1)} collective-permute-done((f32[16,1,512,4]{2,3,0,1:T(4,128)S(1)}, f32[16,1,512,4]{2,3,0,1:T(4,128)S(1)}, u32[]{:S(2)}, u32[]{:S(2)}) %collective-permute-start.16) | collective-permute-done | bytes 131104 | tf_op jit(solution)/shard_map/ppermute | solution.py:90
  1816.3 39.7 fusion.67
  1856.0 42.8 multiply_convert_fusion.2
  1956.5 1721.6 %while.63 = (s32[]{:T(128)}, f32[16,1,512,4,128]{4,2,3,0,1:T(8,128)}, f32[16,1,512,128]{3,2,0,1:T(8,128)}, f32[16,1,512,128]{3,2,0,1:T(8,128)}, bf16[16,512,1,12...) while((s32[]{:T(128)}, ...), condition=%wide.region_10.11_spmd.clone, body=%wide.region_9.10_spmd.clone.sunk | while | flops 21665742848 | bytes 798622272 | solution.py:115
  1967.5 195.9 %collective-permute-done.9 = f32[16,1,512,4]{2,3,0,1:T(4,128)S(1)} collective-permute-done((f32[16,1,512,4]{2,3,0,1:T(4,128)S(1)}, f32[16,1,512,4]{2,3,0,1:T(4,128)S(1)}, u32[]{:S(2)}, u32[]{:S(2)}) %collective-permute-start.9) | collective-permute-done | bytes 131104 | tf_op jit(solution)/shard_map/while/body/eval_jaxpr/ppermute | solution.py:57
  2227.8 38.3 multiply_convert_fusion.4
  2281.4 133.6 %collective-permute-done.12 = f32[16,1,512,128]{3,2,0,1:T(8,128)} collective-permute-done((f32[16,1,512,128]{3,2,0,1:T(8,128)}, f32[16,1,512,128]{3,2,0,1:T(8,128)}, u32[]{:S(2)}, u32[]{:S(2)}) %collective-permute-start.12) | collective-permute-done | bytes 4194336 | tf_op jit(solution)/shard_map/while/body/eval_jaxpr/ppermute | solution.py:57
  2459.9 35.4 add_select_fusion.16
  2495.4 35.2 add_select_fusion.14
  2547.0 190.3 %collective-permute-done.9 = f32[16,1,512,4]{2,3,0,1:T(4,128)S(1)} collective-permute-done((f32[16,1,512,4]{2,3,0,1:T(4,128)S(1)}, f32[16,1,512,4]{2,3,0,1:T(4,128)S(1)}, u32[]{:S(2)}, u32[]{:S(2)}) %collective-permute-start.9) | collective-permute-done | bytes 131104 | tf_op jit(solution)/shard_map/while/body/eval_jaxpr/ppermute | solution.py:57
  2803.5 38.3 multiply_convert_fusion.4
  2857.1 131.8 %collective-permute-done.12 = f32[16,1,512,128]{3,2,0,1:T(8,128)} collective-permute-done((f32[16,1,512,128]{3,2,0,1:T(8,128)}, f32[16,1,512,128]{3,2,0,1:T(8,128)}, u32[]{:S(2)}, u32[]{:S(2)}) %collective-permute-start.12) | collective-permute-done | bytes 4194336 | tf_op jit(solution)/shard_map/while/body/eval_jaxpr/ppermute | solution.py:57
  3033.8 35.4 add_select_fusion.16
  3069.3 35.2 add_select_fusion.14
  3122.8 188.5 %collective-permute-done.9 = f32[16,1,512,4]{2,3,0,1:T(4,128)S(1)} collective-permute-done((f32[16,1,512,4]{2,3,0,1:T(4,128)S(1)}, f32[16,1,512,4]{2,3,0,1:T(4,128)S(1)}, u32[]{:S(2)}, u32[]{:S(2)}) %collective-permute-start.9) | collective-permute-done | bytes 131104 | tf_op jit(solution)/shard_map/while/body/eval_jaxpr/ppermute | solution.py:57
  3378.6 38.3 multiply_convert_fusion.4
  3432.2 130.6 %collective-permute-done.12 = f32[16,1,512,128]{3,2,0,1:T(8,128)} collective-permute-done((f32[16,1,512,128]{3,2,0,1:T(8,128)}, f32[16,1,512,128]{3,2,0,1:T(8,128)}, u32[]{:S(2)}, u32[]{:S(2)}) %collective-permute-start.12) | collective-permute-done | bytes 4194336 | tf_op jit(solution)/shard_map/while/body/eval_jaxpr/ppermute | solution.py:57
  3607.8 35.4 add_select_fusion.16
  3643.2 34.6 add_select_fusion.14
  3731.0 40.0 collective-permute-done.19
  3771.0 39.1 fusion.54
  3894.4 307.7 %collective-permute-done.24 = f32[16,1,512,128]{3,2,0,1:T(8,128)} collective-permute-done((f32[16,1,512,128]{3,2,0,1:T(8,128)}, f32[16,1,512,128]{3,2,0,1:T(8,128)}, u32[]{:S(2)}, u32[]{:S(2)}) %collective-permute-start.24) | collective-permute-done | bytes 4194336 | tf_op jit(solution)/shard_map/ppermute | solution.py:121
  4207.3 39.7 collective-permute-done.22
  (272 shorter events, 1186.7 us)
Async XLA Ops:
  109.4 377.1 %collective-permute-start = (f32[16,1,512,4,128]{4,2,3,0,1:T(8,128)}, f32[16,1,512,4,128]{4,2,3,0,1:T(8,128)}, u32[]{:S(2)}, u32[]{:S(2)}) collective-permute-start(f32[16,1,512,4,128]{4,2,3,0,1:T(8,128)} %broadcast_select_fusion.28), channel_id=1, source_target_pairs={{0,1},{1,2},{2,3},{3,4},{4,5},{5,6},{6,7},{7,0}} | collective-permute-start | bytes 50331656 | tf_op jit(solution)/shard_map/while/body/eval_jaxpr/ppermute | solution.py:57
  109.4 320.7 %collective-permute-start.3 = (bf16[16,512,1,4,128]{4,1,3,0,2:T(8,128)(2,1)}, bf16[16,512,1,4,128]{4,1,3,0,2:T(8,128)(2,1)}, u32[]{:S(2)}, u32[]{:S(2)}) collective-permute-start(bf16[16,512,1,4,128]{4,1,3,0,2:T(8,128)(2,1)} %get-tuple-element.1020), channel_id=1, source_target_pairs={{0,1},{1,2},{2,3},{3,4},{4,5},{5,6},{6,7},{7,0}} | collective-permute-start | bytes 25165832 | tf_op jit(solution)/shard_map/while/body/eval_jaxpr/ppermute | solution.py:57
  111.0 293.5 %collective-permute-start.2 = (bf16[16,512,1,128]{3,1,0,2:T(8,128)(2,1)}, bf16[16,512,1,128]{3,1,0,2:T(8,128)(2,1)}, u32[]{:S(2)}, u32[]{:S(2)}) collective-permute-start(bf16[16,512,1,128]{3,1,0,2:T(8,128)(2,1)} %get-tuple-element.1018), channel_id=1, source_target_pairs={{0,1},{1,2},{2,3},{3,4},{4,5},{5,6},{6,7},{7,0}} | collective-permute-start | bytes 6291464 | tf_op jit(solution)/shard_map/while/body/eval_jaxpr/ppermute | solution.py:57
  111.0 316.0 %collective-permute-start.4 = (bf16[16,512,1,128]{3,1,0,2:T(8,128)(2,1)}, bf16[16,512,1,128]{3,1,0,2:T(8,128)(2,1)}, u32[]{:S(2)}, u32[]{:S(2)}) collective-permute-start(bf16[16,512,1,128]{3,1,0,2:T(8,128)(2,1)} %get-tuple-element.1019), channel_id=1, source_target_pairs={{0,1},{1,2},{2,3},{3,4},{4,5},{5,6},{6,7},{7,0}} | collective-permute-start | bytes 6291464 | tf_op jit(solution)/shard_map/while/body/eval_jaxpr/ppermute | solution.py:57
  112.6 373.4 %collective-permute-start.1 = (f32[16,1,512,4]{2,3,0,1:T(4,128)S(1)}, f32[16,1,512,4]{2,3,0,1:T(4,128)S(1)}, u32[]{:S(2)}, u32[]{:S(2)}) collective-permute-start(f32[16,1,512,4]{2,3,0,1:T(4,128)S(1)} %broadcast_select_fusion.29), channel_id=1, source_target_pairs={{0,1},{1,2},{2,3},{3,4},{4,5},{5,6},{6,7},{7,0}} | collective-permute-start | bytes 393224 | tf_op jit(solution)/shard_map/while/body/eval_jaxpr/ppermute | solution.py:57
  544.9 377.1 %collective-permute-start = (f32[16,1,512,4,128]{4,2,3,0,1:T(8,128)}, f32[16,1,512,4,128]{4,2,3,0,1:T(8,128)}, u32[]{:S(2)}, u32[]{:S(2)}) collective-permute-start(f32[16,1,512,4,128]{4,2,3,0,1:T(8,128)} %broadcast_select_fusion.28), channel_id=1, source_target_pairs={{0,1},{1,2},{2,3},{3,4},{4,5},{5,6},{6,7},{7,0}} | collective-permute-start | bytes 50331656 | tf_op jit(solution)/shard_map/while/body/eval_jaxpr/ppermute | solution.py:57
  544.9 320.7 %collective-permute-start.3 = (bf16[16,512,1,4,128]{4,1,3,0,2:T(8,128)(2,1)}, bf16[16,512,1,4,128]{4,1,3,0,2:T(8,128)(2,1)}, u32[]{:S(2)}, u32[]{:S(2)}) collective-permute-start(bf16[16,512,1,4,128]{4,1,3,0,2:T(8,128)(2,1)} %get-tuple-element.1020), channel_id=1, source_target_pairs={{0,1},{1,2},{2,3},{3,4},{4,5},{5,6},{6,7},{7,0}} | collective-permute-start | bytes 25165832 | tf_op jit(solution)/shard_map/while/body/eval_jaxpr/ppermute | solution.py:57
  547.4 292.6 %collective-permute-start.2 = (bf16[16,512,1,128]{3,1,0,2:T(8,128)(2,1)}, bf16[16,512,1,128]{3,1,0,2:T(8,128)(2,1)}, u32[]{:S(2)}, u32[]{:S(2)}) collective-permute-start(bf16[16,512,1,128]{3,1,0,2:T(8,128)(2,1)} %get-tuple-element.1018), channel_id=1, source_target_pairs={{0,1},{1,2},{2,3},{3,4},{4,5},{5,6},{6,7},{7,0}} | collective-permute-start | bytes 6291464 | tf_op jit(solution)/shard_map/while/body/eval_jaxpr/ppermute | solution.py:57
  547.5 315.1 %collective-permute-start.4 = (bf16[16,512,1,128]{3,1,0,2:T(8,128)(2,1)}, bf16[16,512,1,128]{3,1,0,2:T(8,128)(2,1)}, u32[]{:S(2)}, u32[]{:S(2)}) collective-permute-start(bf16[16,512,1,128]{3,1,0,2:T(8,128)(2,1)} %get-tuple-element.1019), channel_id=1, source_target_pairs={{0,1},{1,2},{2,3},{3,4},{4,5},{5,6},{6,7},{7,0}} | collective-permute-start | bytes 6291464 | tf_op jit(solution)/shard_map/while/body/eval_jaxpr/ppermute | solution.py:57
  548.2 373.4 %collective-permute-start.1 = (f32[16,1,512,4]{2,3,0,1:T(4,128)S(1)}, f32[16,1,512,4]{2,3,0,1:T(4,128)S(1)}, u32[]{:S(2)}, u32[]{:S(2)}) collective-permute-start(f32[16,1,512,4]{2,3,0,1:T(4,128)S(1)} %broadcast_select_fusion.29), channel_id=1, source_target_pairs={{0,1},{1,2},{2,3},{3,4},{4,5},{5,6},{6,7},{7,0}} | collective-permute-start | bytes 393224 | tf_op jit(solution)/shard_map/while/body/eval_jaxpr/ppermute | solution.py:57
  980.5 376.4 %collective-permute-start = (f32[16,1,512,4,128]{4,2,3,0,1:T(8,128)}, f32[16,1,512,4,128]{4,2,3,0,1:T(8,128)}, u32[]{:S(2)}, u32[]{:S(2)}) collective-permute-start(f32[16,1,512,4,128]{4,2,3,0,1:T(8,128)} %broadcast_select_fusion.28), channel_id=1, source_target_pairs={{0,1},{1,2},{2,3},{3,4},{4,5},{5,6},{6,7},{7,0}} | collective-permute-start | bytes 50331656 | tf_op jit(solution)/shard_map/while/body/eval_jaxpr/ppermute | solution.py:57
  980.5 320.7 %collective-permute-start.3 = (bf16[16,512,1,4,128]{4,1,3,0,2:T(8,128)(2,1)}, bf16[16,512,1,4,128]{4,1,3,0,2:T(8,128)(2,1)}, u32[]{:S(2)}, u32[]{:S(2)}) collective-permute-start(bf16[16,512,1,4,128]{4,1,3,0,2:T(8,128)(2,1)} %get-tuple-element.1020), channel_id=1, source_target_pairs={{0,1},{1,2},{2,3},{3,4},{4,5},{5,6},{6,7},{7,0}} | collective-permute-start | bytes 25165832 | tf_op jit(solution)/shard_map/while/body/eval_jaxpr/ppermute | solution.py:57
  983.9 291.7 %collective-permute-start.2 = (bf16[16,512,1,128]{3,1,0,2:T(8,128)(2,1)}, bf16[16,512,1,128]{3,1,0,2:T(8,128)(2,1)}, u32[]{:S(2)}, u32[]{:S(2)}) collective-permute-start(bf16[16,512,1,128]{3,1,0,2:T(8,128)(2,1)} %get-tuple-element.1018), channel_id=1, source_target_pairs={{0,1},{1,2},{2,3},{3,4},{4,5},{5,6},{6,7},{7,0}} | collective-permute-start | bytes 6291464 | tf_op jit(solution)/shard_map/while/body/eval_jaxpr/ppermute | solution.py:57
  983.9 314.2 %collective-permute-start.4 = (bf16[16,512,1,128]{3,1,0,2:T(8,128)(2,1)}, bf16[16,512,1,128]{3,1,0,2:T(8,128)(2,1)}, u32[]{:S(2)}, u32[]{:S(2)}) collective-permute-start(bf16[16,512,1,128]{3,1,0,2:T(8,128)(2,1)} %get-tuple-element.1019), channel_id=1, source_target_pairs={{0,1},{1,2},{2,3},{3,4},{4,5},{5,6},{6,7},{7,0}} | collective-permute-start | bytes 6291464 | tf_op jit(solution)/shard_map/while/body/eval_jaxpr/ppermute | solution.py:57
  984.0 372.6 %collective-permute-start.1 = (f32[16,1,512,4]{2,3,0,1:T(4,128)S(1)}, f32[16,1,512,4]{2,3,0,1:T(4,128)S(1)}, u32[]{:S(2)}, u32[]{:S(2)}) collective-permute-start(f32[16,1,512,4]{2,3,0,1:T(4,128)S(1)} %broadcast_select_fusion.29), channel_id=1, source_target_pairs={{0,1},{1,2},{2,3},{3,4},{4,5},{5,6},{6,7},{7,0}} | collective-permute-start | bytes 393224 | tf_op jit(solution)/shard_map/while/body/eval_jaxpr/ppermute | solution.py:57
  1421.2 395.1 %collective-permute-start.17 = (f32[16,1,512,4,128]{2,4,3,0,1:T(8,128)}, f32[16,1,512,4,128]{2,4,3,0,1:T(8,128)}, u32[]{:S(2)}, u32[]{:S(2)}) collective-permute-start(f32[16,1,512,4,128]{2,4,3,0,1:T(8,128)} %copy.23), channel_id=1, source_target_pairs={{0,5},{1,6},{2,7},{3,0},{4,1},{5,2},{6,3},{7,4}} | collective-permute-start | bytes 50331656 | tf_op jit(solution)/shard_map/ppermute | solution.py:90
  1423.1 361.5 %collective-permute-start.16 = (f32[16,1,512,4]{2,3,0,1:T(4,128)S(1)}, f32[16,1,512,4]{2,3,0,1:T(4,128)S(1)}, u32[]{:S(2)}, u32[]{:S(2)}) collective-permute-start(f32[16,1,512,4]{2,3,0,1:T(4,128)S(1)} %get-tuple-element.538), channel_id=1, source_target_pairs={{0,5},{1,6},{2,7},{3,0},{4,1},{5,2},{6,3},{7,4}} | collective-permute-start | bytes 393224 | tf_op jit(solution)/shard_map/ppermute | solution.py:90
  1430.6 385.6 %collective-permute-start.15 = (bf16[16,512,1,128]{1,3,0,2:T(8,128)(2,1)}, bf16[16,512,1,128]{1,3,0,2:T(8,128)(2,1)}, u32[]{:S(2)}, u32[]{:S(2)}) collective-permute-start(bf16[16,512,1,128]{1,3,0,2:T(8,128)(2,1)} %copy.20), channel_id=1, source_target_pairs={{0,1},{1,2},{2,3},{3,4},{4,5},{5,6},{6,7},{7,0}} | collective-permute-start | bytes 6291464 | tf_op jit(solution)/shard_map/ppermute | solution.py:57
  1959.4 268.4 %collective-permute-start.10 = (bf16[16,512,1,4,128]{4,1,3,0,2:T(8,128)(2,1)}, bf16[16,512,1,4,128]{4,1,3,0,2:T(8,128)(2,1)}, u32[]{:S(2)}, u32[]{:S(2)}) collective-permute-start(bf16[16,512,1,4,128]{4,1,3,0,2:T(8,128)(2,1)} %get-tuple-element.1074), channel_id=1, source_target_pairs={{0,1},{1,2},{2,3},{3,4},{4,5},{5,6},{6,7},{7,0}} | collective-permute-start | bytes 25165832 | tf_op jit(solution)/shard_map/while/body/eval_jaxpr/ppermute | solution.py:57
  2187.3 308.1 %collective-permute-start.5 = (f32[16,1,512,4,128]{4,2,3,0,1:T(8,128)}, f32[16,1,512,4,128]{4,2,3,0,1:T(8,128)}, u32[]{:S(2)}, u32[]{:S(2)}) collective-permute-start(f32[16,1,512,4,128]{4,2,3,0,1:T(8,128)} %broadcast_select_fusion.33), channel_id=1, source_target_pairs={{0,1},{1,2},{2,3},{3,4},{4,5},{5,6},{6,7},{7,0}} | collective-permute-start | bytes 50331656 | tf_op jit(solution)/shard_map/while/body/eval_jaxpr/ppermute | solution.py:57
  2197.8 262.1 %collective-permute-start.13 = (f32[16,1,512,128]{3,2,0,1:T(8,128)}, f32[16,1,512,128]{3,2,0,1:T(8,128)}, u32[]{:S(2)}, u32[]{:S(2)}) collective-permute-start(f32[16,1,512,128]{3,2,0,1:T(8,128)} %broadcast_select_fusion.35), channel_id=1, source_target_pairs={{0,1},{1,2},{2,3},{3,4},{4,5},{5,6},{6,7},{7,0}} | collective-permute-start | bytes 12582920 | tf_op jit(solution)/shard_map/while/body/eval_jaxpr/ppermute | solution.py:57
  2530.7 246.0 %collective-permute-start.6 = (bf16[16,512,1,4,128]{4,1,3,0,2:T(8,128)(2,1)}, bf16[16,512,1,4,128]{4,1,3,0,2:T(8,128)(2,1)}, u32[]{:S(2)}, u32[]{:S(2)}) collective-permute-start(bf16[16,512,1,4,128]{4,1,3,0,2:T(8,128)(2,1)} %get-tuple-element.1073), channel_id=1, source_target_pairs={{0,1},{1,2},{2,3},{3,4},{4,5},{5,6},{6,7},{7,0}} | collective-permute-start | bytes 25165832 | tf_op jit(solution)/shard_map/while/body/eval_jaxpr/ppermute | solution.py:57
  2531.7 271.8 %collective-permute-start.10 = (bf16[16,512,1,4,128]{4,1,3,0,2:T(8,128)(2,1)}, bf16[16,512,1,4,128]{4,1,3,0,2:T(8,128)(2,1)}, u32[]{:S(2)}, u32[]{:S(2)}) collective-permute-start(bf16[16,512,1,4,128]{4,1,3,0,2:T(8,128)(2,1)} %get-tuple-element.1074), channel_id=1, source_target_pairs={{0,1},{1,2},{2,3},{3,4},{4,5},{5,6},{6,7},{7,0}} | collective-permute-start | bytes 25165832 | tf_op jit(solution)/shard_map/while/body/eval_jaxpr/ppermute | solution.py:57
  2761.2 308.1 %collective-permute-start.5 = (f32[16,1,512,4,128]{4,2,3,0,1:T(8,128)}, f32[16,1,512,4,128]{4,2,3,0,1:T(8,128)}, u32[]{:S(2)}, u32[]{:S(2)}) collective-permute-start(f32[16,1,512,4,128]{4,2,3,0,1:T(8,128)} %broadcast_select_fusion.33), channel_id=1, source_target_pairs={{0,1},{1,2},{2,3},{3,4},{4,5},{5,6},{6,7},{7,0}} | collective-permute-start | bytes 50331656 | tf_op jit(solution)/shard_map/while/body/eval_jaxpr/ppermute | solution.py:57
  2773.5 260.3 %collective-permute-start.13 = (f32[16,1,512,128]{3,2,0,1:T(8,128)}, f32[16,1,512,128]{3,2,0,1:T(8,128)}, u32[]{:S(2)}, u32[]{:S(2)}) collective-permute-start(f32[16,1,512,128]{3,2,0,1:T(8,128)} %broadcast_select_fusion.35), channel_id=1, source_target_pairs={{0,1},{1,2},{2,3},{3,4},{4,5},{5,6},{6,7},{7,0}} | collective-permute-start | bytes 12582920 | tf_op jit(solution)/shard_map/while/body/eval_jaxpr/ppermute | solution.py:57
  3104.6 247.8 %collective-permute-start.6 = (bf16[16,512,1,4,128]{4,1,3,0,2:T(8,128)(2,1)}, bf16[16,512,1,4,128]{4,1,3,0,2:T(8,128)(2,1)}, u32[]{:S(2)}, u32[]{:S(2)}) collective-permute-start(bf16[16,512,1,4,128]{4,1,3,0,2:T(8,128)(2,1)} %get-tuple-element.1073), channel_id=1, source_target_pairs={{0,1},{1,2},{2,3},{3,4},{4,5},{5,6},{6,7},{7,0}} | collective-permute-start | bytes 25165832 | tf_op jit(solution)/shard_map/while/body/eval_jaxpr/ppermute | solution.py:57
  3107.4 271.1 %collective-permute-start.10 = (bf16[16,512,1,4,128]{4,1,3,0,2:T(8,128)(2,1)}, bf16[16,512,1,4,128]{4,1,3,0,2:T(8,128)(2,1)}, u32[]{:S(2)}, u32[]{:S(2)}) collective-permute-start(bf16[16,512,1,4,128]{4,1,3,0,2:T(8,128)(2,1)} %get-tuple-element.1074), channel_id=1, source_target_pairs={{0,1},{1,2},{2,3},{3,4},{4,5},{5,6},{6,7},{7,0}} | collective-permute-start | bytes 25165832 | tf_op jit(solution)/shard_map/while/body/eval_jaxpr/ppermute | solution.py:57
  3335.1 308.1 %collective-permute-start.5 = (f32[16,1,512,4,128]{4,2,3,0,1:T(8,128)}, f32[16,1,512,4,128]{4,2,3,0,1:T(8,128)}, u32[]{:S(2)}, u32[]{:S(2)}) collective-permute-start(f32[16,1,512,4,128]{4,2,3,0,1:T(8,128)} %broadcast_select_fusion.33), channel_id=1, source_target_pairs={{0,1},{1,2},{2,3},{3,4},{4,5},{5,6},{6,7},{7,0}} | collective-permute-start | bytes 50331656 | tf_op jit(solution)/shard_map/while/body/eval_jaxpr/ppermute | solution.py:57
  3349.2 258.5 %collective-permute-start.13 = (f32[16,1,512,128]{3,2,0,1:T(8,128)}, f32[16,1,512,128]{3,2,0,1:T(8,128)}, u32[]{:S(2)}, u32[]{:S(2)}) collective-permute-start(f32[16,1,512,128]{3,2,0,1:T(8,128)} %broadcast_select_fusion.35), channel_id=1, source_target_pairs={{0,1},{1,2},{2,3},{3,4},{4,5},{5,6},{6,7},{7,0}} | collective-permute-start | bytes 12582920 | tf_op jit(solution)/shard_map/while/body/eval_jaxpr/ppermute | solution.py:57
  3704.5 546.5 %collective-permute-start.20 = (f32[16,1,512,4,128]{2,4,3,0,1:T(8,128)}, f32[16,1,512,4,128]{2,4,3,0,1:T(8,128)}, u32[]{:S(2)}, u32[]{:S(2)}) collective-permute-start(f32[16,1,512,4,128]{2,4,3,0,1:T(8,128)} %copy.43), channel_id=1, source_target_pairs={{0,5},{1,6},{2,7},{3,0},{4,1},{5,2},{6,3},{7,4}} | collective-permute-start | bytes 50331656 | tf_op jit(solution)/shard_map/ppermute | solution.py:122
  3839.9 362.2 %collective-permute-start.24 = (f32[16,1,512,128]{3,2,0,1:T(8,128)}, f32[16,1,512,128]{3,2,0,1:T(8,128)}, u32[]{:S(2)}, u32[]{:S(2)}) collective-permute-start(f32[16,1,512,128]{3,2,0,1:T(8,128)} %add_select_fusion.7), channel_id=1, source_target_pairs={{0,4},{1,5},{2,6},{3,7},{4,0},{5,1},{6,2},{7,3}} | collective-permute-start | bytes 12582920 | tf_op jit(solution)/shard_map/ppermute | solution.py:121
  3863.1 383.9 %collective-permute-start.22 = (f32[16,1,512,128]{3,2,0,1:T(8,128)}, f32[16,1,512,128]{3,2,0,1:T(8,128)}, u32[]{:S(2)}, u32[]{:S(2)}) collective-permute-start(f32[16,1,512,128]{3,2,0,1:T(8,128)} %add_select_fusion.8), channel_id=1, source_target_pairs={{0,4},{1,5},{2,6},{3,7},{4,0},{5,1},{6,2},{7,3}} | collective-permute-start | bytes 12582920 | tf_op jit(solution)/shard_map/ppermute | solution.py:121
  (57 other events, 7393.0 us)
where the time goes:
time: 4300 us; the launch traced here: 4290 us
  waiting for transfers between devices  2670 us (62%)
  matrix products  1070 us (25%)
  local copies, waits for them, and re-layouts  292 us (7%)
  other arithmetic  191 us (4%)
  starting transfers between devices  64.3 us (1%)
    ppermute x48, waiting for transfers between devices, send_next(): return lax.ppermute(tree_in, CTX_AXES, next_perm)  2210 us
    ppermute x2, waiting for transfers between devices, local_attn(): dk_buf, dv_buf = lax.ppermute((dk_buf, dv_buf), CTX_AXES, home_kv)  347 us
    dot_general x5, matrix products, pair_forward(): jnp.einsum('bhqgk,bkhd->bhqgd', prob_blk.astype(jnp.bfloat16), v_blk, pre...  213 us
    dot_general x5, matrix products, pair_backward(): jnp.einsum('bqhgd,bkhd->bhqgk', do_blk, v_blk, preferred_element_type=jnp...  197 us
    dot_general x5, matrix products, pair_backward(): jnp.einsum('bhqgk,bqhgd->bhkd', prob_blk.astype(jnp.bfloat16), do_blk, pr...  167 us
    dot_general x5, matrix products, pair_backward(): jnp.einsum('bhqgk,bkhd->bhqgd', score_grad, k_blk, preferred_element_type...  153 us
    dot_general x5, matrix products, pair_forward(): jnp.einsum('bqhgd,bkhd->bhqgk', q_blk, k_blk, preferred_element_type=jnp....  134 us
    while x81, local copies, waits for them, and re-layouts  111 us
  transfers between devices with their start and end apart: 53, of which 23 were waited for; matrix products, arithmetic and copies ran while one was open for 23% of the time, Pallas kernels for 0%

commit v1 on v0

v1 whole, which is shorter than its diff:
```python
import functools
import math

import jax
import jax.numpy as jnp
from jax import lax
from jax.experimental import pallas as pl
from jax.experimental.pallas import tpu as pltpu
from jax.sharding import PartitionSpec as P

MESH = pl.DeviceIdType.MESH
NT = (((1,), (1,)), ((), ()))
F32 = jnp.float32
BF16 = jnp.bfloat16
NDEV = 8
BLK = 512
QR = 4 * BLK
HD = 128
SEQ = NDEV * BLK
SCALE = 1.0 / math.sqrt(HD)
SCALE2 = SCALE * math.log2(math.e)
DIAG = 256
RA = 1024
RB = 1024
RC = 1024
NSLOT = 4


def lane_fold(op, s):
    acc = s[:, 0:128]
    for g in range(1, s.shape[1] // 128):
        acc = op(acc, s[:, g * 128:(g + 1) * 128])
    return acc


def lanes(x, width):
    return jnp.tile(x, (1, width // 128))


def attn_tile(blk, slot, oslot, kv, qb, dob, kb, vb, ob, dqb, S, dkt, dvt, oacc, dqacc, mx, lx, qT, doT, after_forward, before_pass_c):
    own = pl.multiple_of(blk * BLK, BLK)
    blocks = lambda n: [(r, n) for r in range(0, QR, n)]

    def diag(fn):
        for u in reversed(range(BLK // DIAG)):
            fn(u, DIAG * (u + 1), u * DIAG * 4, DIAG * 4)

    def score_diag(u, w, r, n):
        rs = pl.ds(r, n)
        s = lax.dot_general(qb[slot, rs, :], kb[kv, pl.ds(own, w), :], NT, preferred_element_type=F32)
        row = lax.broadcasted_iota(jnp.int32, (n, DIAG), 0) // 4
        col = lax.broadcasted_iota(jnp.int32, (n, DIAG), 1)
        sd = jnp.where(row >= col, s[:, w - DIAG:], -1e30)
        S[rs, pl.ds(own + (w - DIAG), DIAG)] = sd
        m = lane_fold(jnp.maximum, sd)
        if w > DIAG:
            S[rs, pl.ds(own, w - DIAG)] = s[:, :w - DIAG]
            m = jnp.maximum(m, lane_fold(jnp.maximum, s[:, :w - DIAG]))
        mx[rs, :] = m

    diag(score_diag)
    qT[...] = qb[slot].T
    doT[...] = dob[slot].T

    @pl.loop(0, blk)
    def _(j):
        o = pl.multiple_of(j * BLK, BLK)
        for r, n in blocks(RA):
            rs = pl.ds(r, n)
            s = lax.dot_general(qb[slot, rs, :], kb[kv, pl.ds(o, BLK), :], NT, preferred_element_type=F32)
            S[rs, pl.ds(o, BLK)] = s
            mx[rs, :] = jnp.maximum(mx[rs, :], lane_fold(jnp.maximum, s))

    mx[...] = jnp.broadcast_to(jnp.max(mx[...], axis=1, keepdims=True) * SCALE2, (QR, 128))

    def probs(o, w, r, n, first):
        rs = pl.ds(r, n)
        p = jnp.exp2(S[rs, pl.ds(o, w)] * SCALE2 - lanes(mx[rs, :], w))
        S[rs, pl.ds(o, w)] = p
        ls = lane_fold(jnp.add, p)
        oo = jnp.dot(p.astype(BF16), vb[kv, pl.ds(o, w), :], preferred_element_type=F32)
        if first:
            lx[rs, :] = ls
            oacc[rs, :] = oo
        else:
            lx[rs, :] += ls
            oacc[rs, :] += oo

    diag(lambda u, w, r, n: probs(own, w, r, n, True))

    @pl.loop(0, blk)
    def _(j):
        o = pl.multiple_of(j * BLK, BLK)
        for r, n in blocks(RB):
            probs(o, BLK, r, n, False)

    lx[...] = jnp.broadcast_to(1.0 / jnp.sum(lx[...], axis=1, keepdims=True), (QR, 128))
    out = oacc[...] * lx[...]
    ob[oslot] = out.astype(BF16)
    mx[...] = jnp.broadcast_to(jnp.sum(out * dob[slot].astype(F32), axis=1, keepdims=True), (QR, 128))
    after_forward()
    before_pass_c()

    def grads(o, w, r, n):
        rs = pl.ds(r, n)
        pn = S[rs, pl.ds(o, w)] * lanes(lx[rs, :], w)
        gv = jnp.dot(doT[:, rs], pn.astype(BF16), preferred_element_type=F32)
        dp = lax.dot_general(dob[slot, rs, :], vb[kv, pl.ds(o, w), :], NT, preferred_element_type=F32)
        ds = (pn * (dp - lanes(mx[rs, :], w))).astype(BF16)
        gk = jnp.dot(qT[:, rs], ds, preferred_element_type=F32)
        gq = jnp.dot(ds, kb[kv, pl.ds(o, w), :], preferred_element_type=F32)
        return gv, gk, gq

    def grads_diag(u, w, r, n):
        gv, gk, gq = grads(own, w, r, n)
        dqacc[pl.ds(r, n), :] = gq
        dvt[:, pl.ds(own, w)] += gv
        dkt[:, pl.ds(own, w)] += gk

    diag(grads_diag)

    @pl.loop(0, blk)
    def _(j):
        o = pl.multiple_of(j * BLK, BLK)
        av, ak = None, None
        for r, n in blocks(RC):
            gv, gk, gq = grads(o, BLK, r, n)
            dqacc[pl.ds(r, n), :] += gq
            av = gv if av is None else av + gv
            ak = gk if ak is None else ak + gk
        dvt[:, pl.ds(o, BLK)] += av
        dkt[:, pl.ds(o, BLK)] += ak

    dqb[oslot] = (dqacc[...] * SCALE).astype(BF16)


def kernel(q, do, k, v, out, dq, dk, dv, qr, dor, kr, vr,
           qb, dob, kb, vb, ob, dqb, kst, vst, S, dkt, dvt, oacc, dqacc, mx, lx, qT, doT,
           send, recv, rsend, rrecv, load, lout):
    y = lax.axis_index('ctxo')
    b = lax.axis_index('ctx')
    x = b // 2
    core = lax.rem(b, 2)
    me = y * 4 + b

    def device(d):
        return (0, d // 4, lax.rem(d, 4))

    def partner(step):
        off = lax.rem(2 * step, NDEV) + step // 4
        return (lax.rem(y + off // 4, 2) * 4 + lax.rem(x + lax.rem(off // 2, 2), 2) * 2
                + lax.rem(core + lax.rem(off, 2), 2))

    barrier = pltpu.get_barrier_semaphore()
    for step in range(1, NDEV):
        pl.semaphore_signal(barrier, inc=1, device_id=device(partner(step)), device_id_type=MESH)
    pl.semaphore_wait(barrier, NDEV - 1)

    src = (k, v, q, do)
    dst = (kr, vr, qr, dor)

    def ship(t, rr, step):
        h = partner(step)
        return pltpu.make_async_remote_copy(
            src_ref=src[t].at[2 * h + rr], dst_ref=dst[t].at[rr, me],
            send_sem=send.at[t, rr, step], recv_sem=recv.at[t, rr, me],
            device_id=device(h), device_id_type=MESH)

    def arrival(t, rr, i):
        return pltpu.make_async_remote_copy(
            src_ref=src[t].at[0], dst_ref=dst[t].at[rr, i],
            send_sem=send.at[t, rr, 0], recv_sem=recv.at[t, rr, i],
            device_id=device(partner(1)), device_id_type=MESH)

    @pl.loop(1, NDEV)
    def _(step):
        ship(0, 0, step).start()
        ship(1, 0, step).start()

    @pl.loop(1, NDEV)
    def _(step):
        ship(2, 0, step).start()
        ship(3, 0, step).start()

    bufs = (kb, vb, qb, dob)

    def kv_copies(rr, i, own):
        o = pl.ds(pl.multiple_of(i * BLK, BLK), BLK)
        for t in range(2):
            source = src[t].at[2 * me + rr] if own else dst[t].at[rr, i]
            yield pltpu.make_async_copy(source, bufs[t].at[rr, o, :], load.at[t, i])

    def fetch_kv(rr):
        for c in kv_copies(rr, me, True):
            c.start()

        @pl.loop(1, NDEV)
        def _(step):
            i = partner(step)
            arrival(0, rr, i).wait_recv()
            arrival(1, rr, i).wait_recv()
            for c in kv_copies(rr, i, False):
                c.start()

        @pl.loop(0, NDEV)
        def _(i):
            for c in kv_copies(rr, i, False):
                c.wait()

    def fetch(rr, step, slot):
        i = partner(step)

        @pl.when(step == 0)
        def _():
            for t in (2, 3):
                pltpu.make_async_copy(src[t].at[2 * me + rr], bufs[t].at[slot], load.at[t, 0]).start()

        @pl.when(step != 0)
        def _():
            for t in (2, 3):
                arrival(t, rr, i).wait_recv()
                pltpu.make_async_copy(dst[t].at[rr, i], bufs[t].at[slot], load.at[t, 0]).start()

    def fetch_wait(rr, step, slot):
        for t in (2, 3):
            pltpu.make_async_copy(dst[t].at[rr, partner(step)], bufs[t].at[slot], load.at[t, 0]).wait()

    rbuf = (ob, dqb, kst, vst)
    rdst = (out, dq, dk, dv)

    def reply(t, task):
        rr = task // NDEV
        i = partner(lax.rem(task, NDEV))
        if t < 2:
            idx = lax.rem(task, NSLOT)
            source = rbuf[t].at[idx]
        else:
            idx = i
            source = rbuf[t].at[pl.ds(pl.multiple_of(i * BLK, BLK), BLK), :]
        row = 2 * me + rr
        remote = pltpu.make_async_remote_copy(
            src_ref=source, dst_ref=rdst[t].at[row],
            send_sem=rsend.at[t, idx], recv_sem=rrecv.at[t, row],
            device_id=device(i), device_id_type=MESH)
        local = pltpu.make_async_copy(source, rdst[t].at[row], lout.at[t])
        return remote, local

    def reply_start(t, task):
        remote, local = reply(t, task)

        @pl.when(lax.rem(task, NDEV) == 0)
        def _():
            local.start()

        @pl.when(lax.rem(task, NDEV) != 0)
        def _():
            remote.start()

    def reply_wait(t, task):
        remote, local = reply(t, task)

        @pl.when(lax.rem(task, NDEV) == 0)
        def _():
            local.wait()

        @pl.when(lax.rem(task, NDEV) != 0)
        def _():
            remote.wait_send()

    fetch(0, 0, 0)

    @pl.loop(0, 2 * NDEV)
    def _(task):
        rr = task // NDEV
        step = lax.rem(task, NDEV)
        i = partner(step)
        slot = lax.rem(task, 2)
        oslot = lax.rem(task, NSLOT)

        @pl.when(step == 0)
        def _():
            fetch_kv(rr)
            dkt[...] = jnp.zeros_like(dkt)
            dvt[...] = jnp.zeros_like(dvt)

        @pl.when(task == 0)
        def _():
            @pl.loop(1, NDEV)
            def _(s):
                ship(0, 1, s).start()
                ship(1, 1, s).start()

        @pl.when((task > 0) & (task < NDEV))
        def _():
            ship(2, 1, step).start()
            ship(3, 1, step).start()

        fetch_wait(rr, step, slot)

        def after_forward():
            reply_start(0, task)

        def before_pass_c():
            @pl.when(task + 1 < 2 * NDEV)
            def _():
                fetch((task + 1) // NDEV, lax.rem(task + 1, NDEV), lax.rem(task + 1, 2))

        @pl.when(task >= NSLOT)
        def _():
            reply_wait(0, task - NSLOT)
            reply_wait(1, task - NSLOT)

        attn_tile(i, slot, oslot, rr, qb, dob, kb, vb, ob, dqb, S, dkt, dvt, oacc, dqacc, mx, lx, qT, doT,
                  after_forward, before_pass_c)
        reply_start(1, task)

        @pl.when(step == NDEV - 1)
        def _():
            @pl.when(rr > 0)
            def _():
                @pl.loop(0, NDEV)
                def _(s):
                    reply_wait(2, s)
                    reply_wait(3, s)

            @pl.loop(0, NDEV)
            def _(s):
                o = pl.multiple_of(partner(s) * BLK, BLK)
                kst[pl.ds(o, BLK), :] = (dkt[:, pl.ds(o, BLK)] * SCALE).T.astype(BF16)
                vst[pl.ds(o, BLK), :] = dvt[:, pl.ds(o, BLK)].T.astype(BF16)
                reply_start(2, rr * NDEV + s)
                reply_start(3, rr * NDEV + s)

    @pl.loop(2 * NDEV - NSLOT, 2 * NDEV)
    def _(task):
        reply_wait(0, task)
        reply_wait(1, task)

    @pl.loop(NDEV, 2 * NDEV)
    def _(task):
        reply_wait(2, task)
        reply_wait(3, task)

    @pl.loop(1, NDEV)
    def _(step):
        for rr in range(2):
            for t in range(4):
                ship(t, rr, step).wait_send()

    @pl.loop(0, 2 * NDEV)
    def _(row):
        @pl.when(row // 2 != me)
        def _():
            for t in range(4):
                source = rbuf[t].at[0] if t < 2 else rbuf[t].at[pl.ds(0, BLK), :]
                pltpu.make_async_remote_copy(
                    src_ref=source, dst_ref=rdst[t].at[row],
                    send_sem=rsend.at[t, 0], recv_sem=rrecv.at[t, row],
                    device_id=device(partner(1)), device_id_type=MESH).wait_recv()


def solution(mesh):
    spec = P('data', ('ctxo', 'ctx'), None, None)
    any_spec = pl.BlockSpec(memory_space=pl.ANY)

    def local_attn(q_in, k_in, v_in, do_in):
        rows = q_in.shape[0]
        wide = jax.ShapeDtypeStruct((rows, QR, HD), BF16)
        narrow = jax.ShapeDtypeStruct((rows, BLK, HD), BF16)
        land_wide = jax.ShapeDtypeStruct((2, NDEV, QR, HD), BF16)
        land_narrow = jax.ShapeDtypeStruct((2, NDEV, BLK, HD), BF16)
        call = pl.pallas_call(
            kernel,
            out_shape=[wide, wide, narrow, narrow, land_wide, land_wide, land_narrow, land_narrow],
            in_specs=[any_spec] * 4,
            out_specs=[any_spec] * 8,
            scratch_shapes=[
                pltpu.VMEM((2, QR, HD), BF16), pltpu.VMEM((2, QR, HD), BF16),
                pltpu.VMEM((2, SEQ, HD), BF16), pltpu.VMEM((2, SEQ, HD), BF16),
                pltpu.VMEM((NSLOT, QR, HD), BF16), pltpu.VMEM((NSLOT, QR, HD), BF16),
                pltpu.VMEM((SEQ, HD), BF16), pltpu.VMEM((SEQ, HD), BF16),
                pltpu.VMEM((QR, SEQ), F32),
                pltpu.VMEM((HD, SEQ), F32), pltpu.VMEM((HD, SEQ), F32),
                pltpu.VMEM((QR, HD), F32), pltpu.VMEM((QR, HD), F32),
                pltpu.VMEM((QR, 128), F32), pltpu.VMEM((QR, 128), F32),
                pltpu.VMEM((HD, QR), BF16), pltpu.VMEM((HD, QR), BF16),
                pltpu.SemaphoreType.DMA((4, 2, NDEV)), pltpu.SemaphoreType.DMA((4, 2, NDEV)),
                pltpu.SemaphoreType.DMA((4, NDEV)), pltpu.SemaphoreType.DMA((4, 2 * NDEV)),
                pltpu.SemaphoreType.DMA((4, NDEV)), pltpu.SemaphoreType.DMA((4,)),
            ],
            compiler_params=pltpu.CompilerParams(
                collective_id=0, has_side_effects=True, vmem_limit_bytes=67043328),
        )
        res = call(q_in.reshape(rows, QR, HD), do_in.reshape(rows, QR, HD),
                   k_in.reshape(rows, BLK, HD), v_in.reshape(rows, BLK, HD))
        return (res[0].reshape(q_in.shape), res[1].reshape(q_in.shape),
                res[2].reshape(k_in.shape), res[3].reshape(v_in.shape))

    return jax.shard_map(local_attn, mesh=mesh, in_specs=(spec,) * 4, out_specs=(spec,) * 4, check_vma=False)
```

time: 4300 us -> 478 us (0.11)
  waiting for transfers between devices: 2670 us -> 0 us
  matrix products: 1070 us -> 0 us
  Pallas kernels: 0 us -> 456 us
  local copies, waits for them, and re-layouts: 292 us -> 16 us
  other arithmetic: 191 us -> 0 us
  starting transfers between devices: 64.3 us -> 0 us
    ppermute x53 -> x0, waiting for transfers between devices: 2670 us -> none  [the longest x48 2210 us: send_next(): return lax.ppermute(tree_in, CTX_AXES, next_perm)]
    dot_general x34 -> x0, matrix products: 1070 us -> none  [the longest x5 213 us: pair_forward(): jnp.einsum('bhqgk,bkhd->bhqgd', prob_blk.astype(jnp.bfloat16), v_blk, pre...]
    pallas_call x0 -> x1, Pallas kernels: none -> 456 us  [local_attn(): call(q_in.reshape(rows, QR, HD), do_in.reshape(rows, QR, HD), k_in.reshap...]
    while x86 -> x0, local copies, waits for them, and re-layouts: 186 us -> none
    reduce_sum x5 -> x0, other arithmetic: 106 us -> none  [pair_forward(): row_sum = jnp.sum(prob_blk, axis=-1)]
    unnamed x33 -> x10, local copies, waits for them, and re-layouts: 106 us -> 16 us
    while x15 -> x0, other arithmetic: 73.5 us -> none
    ppermute x53 -> x0, starting transfers between devices: 64.3 us -> none  [the longest x48 57.8 us: send_next(): return lax.ppermute(tree_in, CTX_AXES, next_perm)]
  transfers between devices with their start and end apart: 53 -> 0, of which waited for: 23 -> 0; matrix products, arithmetic and copies ran while one was open for 23% -> 0% of each run, Pallas kernels for 0% -> 0%
where the time goes in v1:
time: 478 us; the launch traced here: 473 us
  Pallas kernels  456 us (95%)
  local copies, waits for them, and re-layouts  16 us (3%)
    pallas_call x1, Pallas kernels, local_attn(): call(q_in.reshape(rows, QR, HD), do_in.reshape(rows, QR, HD), k_in.reshap...  456 us
    unnamed x10, local copies, waits for them, and re-layouts  16 us

profile of v1, /device:TPU:2, one launch (start us, length us, event | category | flops | bytes accessed | tf_op | source)
XLA Modules:
  0.0 472.5 jit_solution(9267956067962485460)
XLA Ops:
  0.6 455.9 %shard_map.75 = (bf16[16,2048,128]{2,1,0:T(8,128)(2,1)}, bf16[16,2048,128]{2,1,0:T(8,128)(2,1)}, bf16[16,512,128]{2,1,0:T(8,128)(2,1)}, bf16[16,512,128]{2,1,0:T...) custom-call(bf16[16,2048,128]{2,1,0:T(8,128)(2,1)} %bitcast.12, ...), custom_call_target="tpu_custom_call" | custom-call | tf_op jit(solution)/shard_map/pallas_call | solution.py:394
  456.5 0.0 copy-start
  456.5 9.1 %copy.14 = bf16[16,512,4,128]{3,2,1,0:T(4,128)(2,1)} copy(bf16[16,512,4,128]{3,2,1,0:T(4,128)(2,1)} %bitcast.15) | data formatting | bytes 16777216
  465.6 0.0 copy-done
  465.6 0.0 copy-start.2
  465.6 0.0 copy-start.1
  465.6 4.3 copy.15
  469.9 0.0 copy-done.2
  469.9 1.3 copy.16
  471.2 0.0 copy-done.1
  471.2 1.3 copy.17
Async XLA Ops:
  456.5 9.1 %copy-start = (bf16[16,2048,128]{2,1,0:T(8,128)(2,1)S(1)}, bf16[16,2048,128]{2,1,0:T(8,128)(2,1)}, u32[]{:S(2)}) copy-start(bf16[16,2048,128]{2,1,0:T(8,128)(2,1)} %get-tuple-element.9) | copy-start | bytes 25165828
  465.6 4.3 copy-start.2
  465.6 5.6 %copy-start.1 = (bf16[16,512,128]{2,1,0:T(8,128)(2,1)S(1)}, bf16[16,512,128]{2,1,0:T(8,128)(2,1)}, u32[]{:S(2)}) copy-start(bf16[16,512,128]{2,1,0:T(8,128)(2,1)} %get-tuple-element.11) | copy-start | bytes 6291460

commit v2 on v1

v2 whole, which is shorter than its diff:
```python
import functools
import math

import jax
import jax.numpy as jnp
from jax import lax
from jax.experimental import pallas as pl
from jax.experimental.pallas import tpu as pltpu
from jax.sharding import PartitionSpec as P

MESH = pl.DeviceIdType.MESH
NT = (((1,), (1,)), ((), ()))
F32 = jnp.float32
BF16 = jnp.bfloat16
NDEV = 8
BLK = 512
QR = 4 * BLK
HD = 128
SEQ = NDEV * BLK
SCALE = 1.0 / math.sqrt(HD)
SCALE2 = SCALE * math.log2(math.e)
DIAG = 256
RA = 1024
RB = 1024
RC = 1024
NSLOT = 2
NA = 10
NP = NA // 2
DIRECT = 5
HOMES = (0, 0, 1, 2, 4, 5)
HSLOT = (0, 1, 0, 0, 0, 0)
EARLY = (0, 3, 2)
LATER = ((), (), (), (1,), (4, 5))


def lane_fold(op, s):
    acc = s[:, 0:128]
    for g in range(1, s.shape[1] // 128):
        acc = op(acc, s[:, g * 128:(g + 1) * 128])
    return acc


def lanes(x, width):
    return jnp.tile(x, (1, width // 128))


def attn_tile(blk, slot, oslot, kv, qb, dob, kb, vb, ob, dqb, S, acc, aslot, oacc, mx, lx, qT, doT, after_forward, before_pass_c):
    own = pl.multiple_of(blk * BLK, BLK)
    blocks = lambda n: [(r, n) for r in range(0, QR, n)]

    def diag(fn):
        for u in reversed(range(BLK // DIAG)):
            fn(u, DIAG * (u + 1), u * DIAG * 4, DIAG * 4)

    def sweep(chunk):
        @pl.loop(0, blk // 2)
        def _(j):
            chunk(pl.multiple_of(2 * j * BLK, BLK))
            chunk(pl.multiple_of((2 * j + 1) * BLK, BLK))

        @pl.when(lax.rem(blk, 2) == 1)
        def _():
            chunk(pl.multiple_of((blk - 1) * BLK, BLK))

    def score_diag(u, w, r, n):
        rs = pl.ds(r, n)
        s = lax.dot_general(qb[slot, rs, :], kb[kv, pl.ds(own, w), :], NT, preferred_element_type=F32)
        row = lax.broadcasted_iota(jnp.int32, (n, DIAG), 0) // 4
        col = lax.broadcasted_iota(jnp.int32, (n, DIAG), 1)
        sd = jnp.where(row >= col, s[:, w - DIAG:], -1e30)
        S[rs, pl.ds(own + (w - DIAG), DIAG)] = sd
        m = lane_fold(jnp.maximum, sd)
        if w > DIAG:
            S[rs, pl.ds(own, w - DIAG)] = s[:, :w - DIAG]
            m = jnp.maximum(m, lane_fold(jnp.maximum, s[:, :w - DIAG]))
        mx[rs, :] = m

    diag(score_diag)
    qT[...] = qb[slot].T
    doT[...] = dob[slot].T

    def chunk_a(o):
        for r, n in blocks(RA):
            rs = pl.ds(r, n)
            s = lax.dot_general(qb[slot, rs, :], kb[kv, pl.ds(o, BLK), :], NT, preferred_element_type=F32)
            S[rs, pl.ds(o, BLK)] = s
            mx[rs, :] = jnp.maximum(mx[rs, :], lane_fold(jnp.maximum, s))

    sweep(chunk_a)

    mx[...] = jnp.broadcast_to(jnp.max(mx[...], axis=1, keepdims=True) * SCALE2, (QR, 128))

    def probs(o, w, r, n, first):
        rs = pl.ds(r, n)
        p = jnp.exp2(S[rs, pl.ds(o, w)] * SCALE2 - lanes(mx[rs, :], w))
        S[rs, pl.ds(o, w)] = p
        ls = lane_fold(jnp.add, p)
        oo = jnp.dot(p.astype(BF16), vb[kv, pl.ds(o, w), :], preferred_element_type=F32)
        if first:
            lx[rs, :] = ls
            oacc[rs, :] = oo
        else:
            lx[rs, :] += ls
            oacc[rs, :] += oo

    diag(lambda u, w, r, n: probs(own, w, r, n, True))

    def chunk_b(o):
        for r, n in blocks(RB):
            probs(o, BLK, r, n, False)

    sweep(chunk_b)

    before_pass_c()
    lx[...] = jnp.broadcast_to(1.0 / jnp.sum(lx[...], axis=1, keepdims=True), (QR, 128))
    out = oacc[...] * lx[...]
    ob[oslot] = out.astype(BF16)
    mx[...] = jnp.broadcast_to(jnp.sum(out * dob[slot].astype(F32), axis=1, keepdims=True), (QR, 128))

    def grads(o, w, r, n, late):
        rs = pl.ds(r, n)

        def upstream():
            return lax.dot_general(dob[slot, rs, :], vb[kv, pl.ds(o, w), :], NT, preferred_element_type=F32)

        if late:
            pn = S[rs, pl.ds(o, w)] * lanes(lx[rs, :], w)
            dp = upstream()
        else:
            dp = upstream()
            pn = S[rs, pl.ds(o, w)] * lanes(lx[rs, :], w)
        ds = (pn * (dp - lanes(mx[rs, :], w))).astype(BF16)
        if late:
            gq = jnp.dot(ds, kb[kv, pl.ds(o, w), :], preferred_element_type=F32)
            gk = jnp.dot(qT[:, rs], ds, preferred_element_type=F32)
            gv = jnp.dot(doT[:, rs], pn.astype(BF16), preferred_element_type=F32)
        else:
            gv = jnp.dot(doT[:, rs], pn.astype(BF16), preferred_element_type=F32)
            gk = jnp.dot(qT[:, rs], ds, preferred_element_type=F32)
            gq = jnp.dot(ds, kb[kv, pl.ds(o, w), :], preferred_element_type=F32)
        return gv, gk, gq

    def grads_diag(u, w, r, n):
        gv, gk, gq = grads(own, w, r, n, False)
        oacc[pl.ds(r, n), :] = gq
        acc[aslot, pl.ds(HD, HD), pl.ds(own, w)] += gv
        acc[aslot, pl.ds(0, HD), pl.ds(own, w)] += gk

    diag(grads_diag)
    after_forward()

    @pl.loop(0, blk)
    def _(j):
        o = pl.multiple_of(j * BLK, BLK)
        av, ak = None, None
        for r, n in blocks(RC):
            gv, gk, gq = grads(o, BLK, r, n, True)
            oacc[pl.ds(r, n), :] += gq
            av = gv if av is None else av + gv
            ak = gk if ak is None else ak + gk
        acc[aslot, pl.ds(HD, HD), pl.ds(o, BLK)] += av
        acc[aslot, pl.ds(0, HD), pl.ds(o, BLK)] += ak

    dqb[oslot] = (oacc[...] * SCALE).astype(BF16)


def kernel(q, do, k, v, out, dq, dk, dv, qh, doh, kh, vh, kn, vn, qs, dos, os_, dqs, dks, dvs, l1, la, lb, lc, pp,
           qb, dob, kb, vb, ob, dqb, kst, vst, fin, S, acc, oacc, mx, lx, qT, doT,
           kvsend, kvrecv, swsend, swrecv, hsend, hrecv, rsend, rrecv, load, lout,
           l1r, lar, lbr, lcr, fl, accin, fsend, tin, tout, osend, asend, ssend):
    y = lax.axis_index('ctxo')
    b = lax.axis_index('ctx')
    x = b // 2
    core = lax.rem(b, 2)
    me = y * 4 + b
    chip = 2 * y + x
    other = 2 * chip + 1 - core

    def device(d):
        return (0, d // 4, lax.rem(d, 4))

    def plane(c):
        return 2 * c + core

    def on_chip(c):
        return pl.when(chip == c)

    def partner(step):
        off = lax.rem(2 * step, NDEV) + step // 4
        return (lax.rem(y + off // 4, 2) * 4 + lax.rem(x + lax.rem(off // 2, 2), 2) * 2
                + lax.rem(core + lax.rem(off, 2), 2))

    def remote(source, target, ssem, rsem, dev):
        return pltpu.make_async_remote_copy(src_ref=source, dst_ref=target, send_sem=ssem, recv_sem=rsem,
                                            device_id=device(dev), device_id_type=MESH)

    barrier = pltpu.get_barrier_semaphore()
    for step in range(1, NDEV):
        pl.semaphore_signal(barrier, inc=1, device_id=device(partner(step)), device_id_type=MESH)
    pl.semaphore_wait(barrier, NDEV - 1)

    src = (k, v, q, do)
    hdst = (kh, vh, qh, doh)
    ndst = (kn, vn)
    sdst = (qs, dos)
    bufs = (kb, vb, qb, dob)

    def kv_send(p, blk, kind, dev, own):
        for t in range(2):
            rows = pl.ds(2 * p, 2)
            source = src[t].at[rows] if own else ndst[t].at[rows, blk]
            yield remote(source, ndst[t].at[rows, blk], kvsend.at[t, p, blk // 2, kind], kvrecv.at[t, p, blk], dev)

    def kv_arrived(p, blk):
        for t in range(2):
            view = ndst[t].at[pl.ds(2 * p, 2), blk]
            remote(view, view, kvsend.at[t, p, 0, 0], kvrecv.at[t, p, blk], other).wait_recv()

    def own_kv(p, what):
        for c, targets in ((0, ((1, 0), (2, 2))), (1, ((3, 0),)), (2, ((3, 0),))):
            @on_chip(c)
            def _():
                for cc, kind in targets:
                    for cp in kv_send(p, me, kind, plane(cc), True):
                        what(cp)
        @pl.when((chip == 1) & (p < DIRECT))
        def _():
            for cp in kv_send(p, me, 2, plane(2), True):
                what(cp)

        for cp in kv_send(p, me, 1, other, True):
            what(cp)

    PASS = {1: ((0, 3),), 2: ((0, None), (1, None)), 3: ((1, 2), (2, None), (0, None))}

    def forward(p, c):
        for cs, relay in PASS[c]:
            blk = plane(cs)
            kv_arrived(p, blk)
            if relay is not None:
                @pl.when((p >= DIRECT) | (c == 1))
                def _():
                    for cp in kv_send(p, blk, 0, plane(relay), False):
                        cp.start()

            for cp in kv_send(p, blk, 1, other, False):
                cp.start()

    def forward_done(p, c):
        for cs, relay in PASS[c]:
            blk = plane(cs)
            if relay is not None:
                @pl.when((p >= DIRECT) | (c == 1))
                def _():
                    for cp in kv_send(p, blk, 0, plane(relay), False):
                        cp.wait_send()

            for cp in kv_send(p, blk, 1, other, False):
                cp.wait_send()

    def swap_send(g):
        for t in range(2):
            yield remote(src[2 + t].at[pl.ds(4 * g + 2, 2)], sdst[t].at[pl.ds(2 * g, 2)],
                         swsend.at[t, g], swrecv.at[t, g], other)

    def home_send(hi):
        for t in range(4):
            yield remote(src[t].at[NA + hi], hdst[t].at[HSLOT[hi], me], hsend.at[t, hi], hrecv.at[t, HSLOT[hi], me],
                         HOMES[hi])

    def home_out(hi, what):
        @pl.when(me != HOMES[hi])
        def _():
            for cp in home_send(hi):
                what(cp)

    start = lambda cp: cp.start()
    own_kv(0, start)

    @pl.when(lax.rem(chip, 2) == 0)
    def _():
        @pl.loop(1, NP)
        def _(p):
            own_kv(p, start)

    home_out(EARLY[0], start)
    for c in (1, 2, 3):
        @on_chip(c)
        def _():
            forward(0, c)

    @pl.when(lax.rem(chip, 2) == 1)
    def _():
        own_kv(1, start)

    for g in range(NP // 2):
        for cp in swap_send(g):
            cp.start()
    for hi in EARLY[1:]:
        home_out(hi, start)

    rbuf = (ob, dqb, kst, vst)
    rdst = (out, dq, dk, dv)

    def reply(t, row, i, idx):
        source = rbuf[t].at[idx]
        far = remote(source, rdst[t].at[row], rsend.at[t, idx], rrecv.at[t, row], i)
        near = pltpu.make_async_copy(source, rdst[t].at[row], lout.at[t, idx])
        return far, near

    def reply_start(t, row, i, idx):
        far, near = reply(t, row, i, idx)

        @pl.when(i == me)
        def _():
            near.start()

        @pl.when(i != me)
        def _():
            far.start()

    def reply_wait(t, row, i, idx):
        far, near = reply(t, row, i, idx)

        @pl.when(i == me)
        def _():
            near.wait()

        @pl.when(i != me)
        def _():
            far.wait_send()

    def tmp(idx):
        return S.at[pl.ds(2 * HD * idx, 2 * HD), pl.ds(0, BLK)]

    def take(source, idx):
        return pltpu.make_async_copy(source, tmp(idx), tin.at[idx])

    def piece(aslot, j):
        return acc.at[aslot, :, pl.ds(pl.multiple_of(j * BLK, BLK), BLK)]

    def pair_out(p, j):
        return remote(piece(0, j), l1.at[p, j], fl.at[0, j], l1r.at[p, j], other)

    def row_keep(p, j):
        return pltpu.make_async_copy(piece(1, j), pp.at[p, j], fl.at[1, j])

    def kept(c):
        return range(6 if c == 3 else 2 * c + 2)

    def row_send(p, c, j):
        target = {3: {0: (la, 0, lar, 1), 1: (la, 1, lar, 1), 2: (la, 2, lar, 1), 3: (la, 3, lar, 1),
                      4: (la, 0, lar, 2), 5: (la, 1, lar, 2)},
                  2: {0: (lb, 0, lbr, 0), 1: (lb, 1, lbr, 0), 2: (la, 0, lar, 3), 3: (la, 1, lar, 3)}}[c]
        land, idx, sem, cc = target[j]
        return remote(pp.at[p, j], land.at[p, idx], osend.at[p, j], sem.at[p, idx], plane(cc))

    SENT = {3: (4, 5, 0, 1), 2: (2, 3, 0, 1)}

    def rows_leave(p):
        for c in range(4):
            @on_chip(c)
            def _():
                for j in kept(c):
                    row_keep(p, j).wait()
                for j in SENT.get(c, ()):
                    if c == 3 and j < 2:
                        @pl.when(p < NP - 1)
                        def _():
                            row_send(p, c, j).start()

                        @pl.when(p == NP - 1)
                        def _():
                            last_direct(j).start()
                    else:
                        row_send(p, c, j).start()
                if c == 1:
                    @pl.when(p == NP - 1)
                    def _():
                        for j in range(2):
                            last_onward(j).start()

    def last_direct(j):
        return remote(pp.at[NP - 1, j], lc.at[j], osend.at[NP - 1, j], lcr.at[j], plane(0))

    def last_onward(j):
        return remote(pp.at[NP - 1, j], la.at[NP - 1, j], osend.at[NP - 1, j], lar.at[NP - 1, j], plane(0))

    def rows_left(p):
        for c, js in ((3, range(6)), (2, range(4))):
            @on_chip(c)
            def _():
                for j in js:
                    row_send(p, c, j).wait_send()

        @pl.when((chip == 1) & (p == NP - 1))
        def _():
            for j in range(2):
                last_onward(j).wait_send()

    def join_chip2(p):
        for j in (2, 3):
            la_arrived(p, j - 2)
            take(pp.at[p, j], 2 * j - 4).start()
            take(la.at[p, j - 2], 2 * j - 3).start()
        for j in (2, 3):
            a, b = 2 * j - 4, 2 * j - 3
            take(pp.at[p, j], a).wait()
            take(la.at[p, j - 2], b).wait()
            tmp(a)[...] += tmp(b)[...]
            pltpu.make_async_copy(tmp(a), pp.at[p, j], tout.at[j - 2]).start()
        for j in (2, 3):
            pltpu.make_async_copy(tmp(2 * j - 4), pp.at[p, j], tout.at[j - 2]).wait()
            row_send(p, 3, j).start()

    def la_arrived(p, j):
        remote(la.at[p, j], la.at[p, j], fl.at[0, 0], lar.at[p, j], other).wait_recv()

    def lb_arrived(p, j):
        remote(lb.at[p, j], lb.at[p, j], fl.at[0, 0], lbr.at[p, j], other).wait_recv()

    def fin_copies(p, kk):
        row = 2 * p + core
        for t in range(2):
            yield (remote(fin.at[kk, t], rdst[2 + t].at[row], fsend.at[kk, t], rrecv.at[2 + t, row], other),
                   pltpu.make_async_copy(fin.at[kk, t], rdst[2 + t].at[row], fsend.at[kk, t]))

    def fin_wait(p, kk):
        for far, near in fin_copies(p, kk):
            @pl.when(core == kk)
            def _():
                near.wait()

            @pl.when(core != kk)
            def _():
                far.wait_send()

    def finish(p, kk, g):
        @pl.when(p > 0)
        def _():
            fin_wait(p - 1, kk)

        fin[kk, 0] = (g[:HD] * SCALE).T.astype(BF16)
        fin[kk, 1] = g[HD:].T.astype(BF16)
        for far, near in fin_copies(p, kk):
            @pl.when(core == kk)
            def _():
                near.start()

            @pl.when(core != kk)
            def _():
                far.start()

    def task_row(task):
        p = task // 2
        row = 2 * p + lax.rem(1 - core + lax.rem(task, 2), 2)
        i = 2 * chip + lax.rem(core + lax.rem(p, 2), 2)
        return row, i

    def kv_slot(t, slot, blk):
        return bufs[t].at[slot, pl.ds(pl.multiple_of(blk * BLK, BLK), BLK), :]

    def fetch(task):
        p = task // 2
        slot = lax.rem(task, 2)
        row, i = task_row(task)

        @pl.when(slot == 0)
        def _():
            @pl.loop(0, chip + 1)
            def _(cs):
                kv_arrived(p, 2 * cs + 1 - core)

            @pl.when(i != me)
            def _():
                for cp in swap_send(p // 2):
                    cp.wait_recv()

        @pl.loop(0, 2 * chip + 2)
        def _(blk):
            @pl.when(blk == me)
            def _():
                for t in range(2):
                    pltpu.make_async_copy(src[t].at[row], kv_slot(t, slot, blk), load.at[t, blk]).start()

            @pl.when(blk != me)
            def _():
                for t in range(2):
                    pltpu.make_async_copy(ndst[t].at[row, blk], kv_slot(t, slot, blk), load.at[t, blk]).start()

        @pl.when(i == me)
        def _():
            for t in (2, 3):
                pltpu.make_async_copy(src[t].at[row], bufs[t].at[slot], load.at[t, 0]).start()

        @pl.when(i != me)
        def _():
            for t in (2, 3):
                pltpu.make_async_copy(sdst[t - 2].at[2 * (p // 2) + lax.rem(row, 2)], bufs[t].at[slot],
                                      load.at[t, 0]).start()

    def fetch_wait(task):
        slot = lax.rem(task, 2)

        @pl.loop(0, 2 * chip + 2)
        def _(blk):
            for t in range(2):
                pltpu.make_async_copy(ndst[t].at[0, blk], kv_slot(t, slot, blk), load.at[t, blk]).wait()

        for t in (2, 3):
            pltpu.make_async_copy(src[t].at[0], bufs[t].at[slot], load.at[t, 0]).wait()

    fetch(0)

    @pl.loop(0, NA)
    def _(task):
        p = task // 2
        slot = lax.rem(task, 2)
        oslot = lax.rem(task, NSLOT)
        row, i = task_row(task)

        @pl.when((task + 2 < NP) & (lax.rem(chip, 2) == 1))
        def _():
            own_kv(task + 2, start)

        for when, rows in enumerate(LATER):
            @pl.when(task == when)
            def _():
                for hi in rows:
                    home_out(hi, start)

        fetch_wait(task)

        @pl.when((slot == 0) & (p > 0))
        def _():
            rows_leave(p - 1)

        @pl.when(task >= NSLOT)
        def _():
            row0, i0 = task_row(task - NSLOT)
            reply_wait(0, row0, i0, oslot)
            reply_wait(1, row0, i0, oslot)

        def after_forward():
            reply_start(0, row, i, oslot)

        def before_pass_c():
            @pl.when((chip == 1) & (task + 1 < NP))
            def _():
                forward(task + 1, 1)

            @pl.when((chip == 2) & (slot == 1) & (p + 1 < NP))
            def _():
                forward(p + 1, 2)

            @pl.when((chip == 3) & (task > 0) & (task < NP))
            def _():
                forward(task, 3)

            @pl.when(task + 1 < NA)
            def _():
                fetch(task + 1)

            @pl.when(slot == 0)
            def _():
                @pl.when(p > 0)
                def _():
                    @pl.loop(0, 2 * chip + 2)
                    def _(j):
                        pair_out(p - 1, j).wait_send()

                acc[0] = jnp.zeros((2 * HD, SEQ), F32)

            @pl.when(slot == 1)
            def _():
                @pl.loop(0, 2 * chip + 2)
                def _(j):
                    pair_out(p, j).wait_recv()
                    pltpu.make_async_copy(l1.at[p, j], piece(1, j), accin.at[j]).start()

                @pl.loop(0, 2 * chip + 2)
                def _(j):
                    pltpu.make_async_copy(l1.at[p, j], piece(1, j), accin.at[j]).wait()

        attn_tile(i, slot, oslot, slot, qb, dob, kb, vb, ob, dqb, S, acc, slot, oacc, mx, lx, qT, doT,
                  after_forward, before_pass_c)
        reply_start(1, row, i, oslot)

        @pl.when(slot == 0)
        def _():
            @pl.loop(0, 2 * chip + 2)
            def _(j):
                pair_out(p, j).start()

        @pl.when((slot == 0) & (p > 0) & (chip == 3))
        def _():
            join_chip2(p - 1)

        @pl.when(slot == 1)
        def _():
            for c in range(4):
                @on_chip(c)
                def _():
                    for j in kept(c):
                        row_keep(p, j).start()
                    if c == 3:
                        for kk in range(2):
                            finish(p, kk, acc[1, :, pl.ds((6 + kk) * BLK, BLK)])

    @pl.loop(NA - NSLOT, NA)
    def _(task):
        row0, i0 = task_row(task)
        reply_wait(0, row0, i0, lax.rem(task, NSLOT))
        reply_wait(1, row0, i0, lax.rem(task, NSLOT))

    @pl.loop(0, 2 * chip + 2)
    def _(j):
        pair_out(NP - 1, j).wait_send()

    rows_leave(NP - 1)

    @on_chip(3)
    def _():
        join_chip2(NP - 1)

    def pick(values):
        got = jnp.int32(values[0])
        for d in range(1, NDEV):
            got = jnp.where(me == d, values[d], got)
        return got

    hcount = pick([HOMES.count(d) for d in range(NDEV)])
    first = pick([HOMES.index(d) if d in HOMES else 0 for d in range(NDEV)])

    def home_block(step):
        return lax.rem(2 * chip - 1 - step + NDEV, NDEV)

    def home_row(h):
        return NA + first + h

    def home_arrived(t, h, i):
        view = hdst[t].at[h, i]
        remote(view, view, hsend.at[t, 0], hrecv.at[t, h, i], other).wait_recv()

    def home_kv(h):
        row = home_row(h)
        for t in range(2):
            pltpu.make_async_copy(src[t].at[row], kv_slot(t, h, me), load.at[t, me]).start()

        @pl.loop(1, NDEV)
        def _(step):
            i = partner(step)
            for t in range(2):
                home_arrived(t, h, i)
                pltpu.make_async_copy(hdst[t].at[h, i], kv_slot(t, h, i), load.at[t, i]).start()

        @pl.loop(0, NDEV)
        def _(i):
            for t in range(2):
                pltpu.make_async_copy(hdst[t].at[h, i], kv_slot(t, h, i), load.at[t, i]).wait()

    def home_fetch(task):
        h = task // NDEV
        step = lax.rem(task, NDEV)
        slot = lax.rem(task, 2)
        i = home_block(step)

        @pl.when(i == me)
        def _():
            for t in (2, 3):
                pltpu.make_async_copy(src[t].at[home_row(h)], bufs[t].at[slot], load.at[t, 0]).start()

        @pl.when(i != me)
        def _():
            for t in (2, 3):
                home_arrived(t, h, i)
                pltpu.make_async_copy(hdst[t].at[h, i], bufs[t].at[slot], load.at[t, 0]).start()

    def home_task(task):
        return home_row(task // NDEV), home_block(lax.rem(task, NDEV))

    stage = (os_, dqs)
    sstage = (dks, dvs)

    def put_down(t, task):
        row, i = home_task(task)
        idx = lax.rem(task, NSLOT)
        return (pltpu.make_async_copy(rbuf[t].at[idx], rdst[t].at[row], lout.at[t, idx]),
                pltpu.make_async_copy(rbuf[t].at[idx], stage[t].at[task], lout.at[t, idx]))

    def put_down_start(t, task):
        own, put = put_down(t, task)
        i = home_task(task)[1]

        @pl.when(i == me)
        def _():
            own.start()

        @pl.when(i != me)
        def _():
            put.start()

    def away(t, task):
        row, i = home_task(task)
        return remote(stage[t].at[task], rdst[t].at[row], asend.at[t, task], rrecv.at[t, row], i)

    def send_away(t, task):
        own, put = put_down(t, task)
        i = home_task(task)[1]

        @pl.when(i == me)
        def _():
            own.wait()

        @pl.when(i != me)
        def _():
            put.wait()
            away(t, task).start()

    def sum_down(t, h, j, away_too):
        target = sstage[t - 2].at[h, j] if away_too else rdst[t].at[home_row(h)]
        return pltpu.make_async_copy(rbuf[t], target, lout.at[t, 0])

    def sum_away(t, h, j):
        row = home_row(h)
        return remote(sstage[t - 2].at[h, j], rdst[t].at[row], ssend.at[t - 2, h, j], rrecv.at[t, row], j)

    @pl.when(hcount > 0)
    def _():
        home_fetch(0)

    @pl.loop(0, NDEV * hcount)
    def _(task):
        h = task // NDEV
        step = lax.rem(task, NDEV)
        slot = lax.rem(task, 2)
        oslot = lax.rem(task, NSLOT)
        row, i = home_task(task)

        @pl.when(step == 0)
        def _():
            home_kv(h)
            acc[h] = jnp.zeros((2 * HD, SEQ), F32)

        for t in (2, 3):
            pltpu.make_async_copy(src[t].at[0], bufs[t].at[slot], load.at[t, 0]).wait()

        @pl.when(task > 0)
        def _():
            send_away(1, task - 1)

        def after_forward():
            put_down_start(0, task)

        def before_pass_c():
            @pl.when(task + 1 < NDEV * hcount)
            def _():
                home_fetch(task + 1)

        attn_tile(i, slot, oslot, h, qb, dob, kb, vb, ob, dqb, S, acc, h, oacc, mx, lx, qT, doT,
                  after_forward, before_pass_c)
        put_down_start(1, task)
        send_away(0, task)

        def flush(j):
            o = pl.ds(pl.multiple_of(j * BLK, BLK), BLK)
            kst[...] = (acc[h, pl.ds(0, HD), o] * SCALE).T.astype(BF16)
            vst[...] = acc[h, pl.ds(HD, HD), o].T.astype(BF16)
            for where, away_too in ((j == me, False), (j != me, True)):
                @pl.when(where)
                def _():
                    for t in (2, 3):
                        sum_down(t, h, j, away_too).start()
                    for t in (2, 3):
                        sum_down(t, h, j, away_too).wait()
                        if away_too:
                            sum_away(t, h, j).start()

        @pl.when(step >= 2 * chip)
        def _():
            flush(i)

        @pl.when(step == NDEV - 1)
        def _():
            @pl.loop(0, 2 * chip)
            def _(j):
                flush(j)

    @pl.when(hcount > 0)
    def _():
        send_away(1, NDEV * hcount - 1)

    @pl.loop(0, NP)
    def _(p):
        @on_chip(1)
        def _():
            def join(j):
                la_arrived(p, j)
                take(pp.at[p, j], 0).start()
                take(la.at[p, j], 1).start()
                take(pp.at[p, j], 0).wait()
                take(la.at[p, j], 1).wait()

            for j in range(2):
                onward = lambda pq: remote(tmp(2 + j), la.at[pq, j], tout.at[j], lar.at[pq, j], plane(0))

                @pl.when(p > 0)
                def _():
                    onward(p - 1).wait_send()

                @pl.when(p < NP - 1)
                def _():
                    join(j)
                    tmp(2 + j)[...] = tmp(0)[...] + tmp(1)[...]
                    onward(p).start()

            for j in (2, 3):
                join(j)
                finish(p, j - 2, tmp(0)[...] + tmp(1)[...])

        @on_chip(2)
        def _():
            for j in range(2):
                la_arrived(p, j)
                take(pp.at[p, 4 + j], 2 * j).start()
                take(la.at[p, j], 2 * j + 1).start()
                take(pp.at[p, 4 + j], 2 * j).wait()
                take(la.at[p, j], 2 * j + 1).wait()
                finish(p, j, tmp(2 * j)[...] + tmp(2 * j + 1)[...])

        @on_chip(0)
        def _():
            for j in range(2):
                la_arrived(p, j)
                lb_arrived(p, j)
                take(pp.at[p, j], 0).start()
                take(la.at[p, j], 1).start()
                take(lb.at[p, j], 2).start()
                take(pp.at[p, j], 0).wait()
                take(la.at[p, j], 1).wait()
                take(lb.at[p, j], 2).wait()

                @pl.when(p == NP - 1)
                def _():
                    remote(lc.at[j], lc.at[j], fl.at[0, 0], lcr.at[j], other).wait_recv()
                    take(lc.at[j], 3).start()
                    take(lc.at[j], 3).wait()
                    tmp(2)[...] += tmp(3)[...]

                finish(p, j, tmp(0)[...] + tmp(1)[...] + tmp(2)[...])

    for kk in range(2):
        fin_wait(NP - 1, kk)

    finished = lambda cp: cp.wait_send()

    @pl.loop(0, NP)
    def _(p):
        own_kv(p, finished)
        rows_left(p)
        for c in (1, 2, 3):
            @on_chip(c)
            def _():
                forward_done(p, c)

    @pl.loop(0, NDEV * hcount)
    def _(task):
        @pl.when(home_task(task)[1] != me)
        def _():
            away(0, task).wait_send()
            away(1, task).wait_send()
            for t in (2, 3):
                sum_away(t, task // NDEV, home_task(task)[1]).wait_send()

    for g in range(NP // 2):
        for cp in swap_send(g):
            cp.wait_send()
    for hi in range(len(HOMES)):
        home_out(hi, finished)

    def came(t, row):
        source = rbuf[t].at[0] if t < 2 else rbuf[t]
        remote(source, rdst[t].at[row], rsend.at[t, 0], rrecv.at[t, row], other).wait_recv()

    for hi in range(len(HOMES)):
        @pl.when(me != HOMES[hi])
        def _():
            for t in range(4):
                came(t, NA + hi)

    @pl.loop(0, NA)
    def _(row):
        @pl.when(lax.rem(row // 2, 2) == 1)
        def _():
            came(0, row)
            came(1, row)

        @pl.when(lax.rem(row, 2) != core)
        def _():
            came(2, row)
            came(3, row)


def solution(mesh):
    spec = P('data', ('ctxo', 'ctx'), None, None)
    any_spec = pl.BlockSpec(memory_space=pl.ANY)

    def local_attn(q_in, k_in, v_in, do_in):
        rows = q_in.shape[0]
        wide = (QR, HD)
        narrow = (BLK, HD)
        shape = lambda lead, tail, dtype=BF16: jax.ShapeDtypeStruct(lead + tail, dtype)
        pair = (2 * HD, BLK)
        vmem = pltpu.VMEM
        dma = pltpu.SemaphoreType.DMA
        call = pl.pallas_call(
            kernel,
            out_shape=[
                shape((rows,), wide), shape((rows,), wide), shape((rows,), narrow), shape((rows,), narrow),
                shape((2, NDEV), wide), shape((2, NDEV), wide), shape((2, NDEV), narrow), shape((2, NDEV), narrow),
                shape((NA, NDEV), narrow), shape((NA, NDEV), narrow), shape((NP,), wide), shape((NP,), wide),
                shape((2 * NDEV,), wide), shape((2 * NDEV,), wide),
                shape((2, NDEV), narrow), shape((2, NDEV), narrow),
                shape((NP, NDEV), pair, F32), shape((NP, 4), pair, F32), shape((NP, 2), pair, F32), shape((2,), pair, F32),
                shape((NP, 6), pair, F32),
            ],
            in_specs=[any_spec] * 4,
            out_specs=[any_spec] * 21,
            scratch_shapes=[
                vmem((2,) + wide, BF16), vmem((2,) + wide, BF16),
                vmem((2, SEQ, HD), BF16), vmem((2, SEQ, HD), BF16),
                vmem((NSLOT,) + wide, BF16), vmem((NSLOT,) + wide, BF16),
                vmem((BLK, HD), BF16), vmem((BLK, HD), BF16),
                vmem((2, 2) + narrow, BF16),
                vmem((QR, SEQ), F32), vmem((2, 2 * HD, SEQ), F32),
                vmem((QR, HD), F32),
                vmem((QR, 128), F32), vmem((QR, 128), F32),
                vmem((HD, QR), BF16), vmem((HD, QR), BF16),
                dma((2, NP, 4, 3)), dma((2, NP, NDEV)), dma((2, NP // 2)), dma((2, NP // 2)),
                dma((4, len(HOMES))), dma((4, 2, NDEV)), dma((2, NSLOT)), dma((4, rows)), dma((4, NDEV)), dma((4, NSLOT)),
                dma((NP, NDEV)), dma((NP, 4)), dma((NP, 2)), dma((2,)), dma((2, NDEV)), dma((NDEV,)), dma((2, 2)),
                dma((4,)), dma((2,)), dma((NP, 6)), dma((2, 2 * NDEV)), dma((2, 2, NDEV)),
            ],
            compiler_params=pltpu.CompilerParams(
                collective_id=0, has_side_effects=True, vmem_limit_bytes=67043328),
        )
        res = call(q_in.reshape((rows,) + wide), do_in.reshape((rows,) + wide),
                   k_in.reshape((rows,) + narrow), v_in.reshape((rows,) + narrow))
        return (res[0].reshape(q_in.shape), res[1].reshape(q_in.shape),
                res[2].reshape(k_in.shape), res[3].reshape(v_in.shape))

    return jax.shard_map(local_attn, mesh=mesh, in_specs=(spec,) * 4, out_specs=(spec,) * 4, check_vma=False)
```

time: 478 us -> 423 us (0.88)
  Pallas kernels: 456 us -> 405 us
    pallas_call x1, Pallas kernels: 456 us -> 405 us  [local_attn(): call(q_in.reshape((rows,) + wide), do_in.reshape((rows,) + wide), k_in.re...]
where the time goes in v2:
time: 423 us; the launch traced here: 422 us
  Pallas kernels  405 us (96%)
  local copies, waits for them, and re-layouts  16 us (4%)
    pallas_call x1, Pallas kernels, local_attn(): call(q_in.reshape((rows,) + wide), do_in.reshape((rows,) + wide), k_in.re...  405 us
    unnamed x10, local copies, waits for them, and re-layouts  16 us

profile of v2, /device:TPU:2, one launch (start us, length us, event | category | flops | bytes accessed | tf_op | source)
XLA Modules:
  0.0 421.5 jit_solution(9927774165117516396)
XLA Ops:
  0.6 404.9 %shard_map.75 = (bf16[16,2048,128]{2,1,0:T(8,128)(2,1)}, bf16[16,2048,128]{2,1,0:T(8,128)(2,1)}, bf16[16,512,128]{2,1,0:T(8,128)(2,1)}, bf16[16,512,128]{2,1,0:T...) custom-call(bf16[16,2048,128]{2,1,0:T(8,128)(2,1)} %bitcast.12, ...), custom_call_target="tpu_custom_call" | custom-call | tf_op jit(solution)/shard_map/pallas_call | solution.py:947
  405.5 0.0 copy-start
  405.5 9.1 %copy.14 = bf16[16,512,4,128]{3,2,1,0:T(4,128)(2,1)} copy(bf16[16,512,4,128]{3,2,1,0:T(4,128)(2,1)} %bitcast.15) | data formatting | bytes 16777216
  414.6 0.0 copy-done
  414.6 0.0 copy-start.2
  414.6 0.0 copy-start.1
  414.6 4.3 %copy.15 = bf16[16,512,4,128]{3,2,1,0:T(4,128)(2,1)} copy(bf16[16,512,4,128]{3,2,1,0:T(4,128)(2,1)S(1)} %bitcast.14) | data formatting | bytes 16777216
  418.9 0.0 copy-done.2
  418.9 1.3 copy.16
  420.2 0.0 copy-done.1
  420.2 1.3 copy.17
Async XLA Ops:
  405.5 9.1 %copy-start = (bf16[16,2048,128]{2,1,0:T(8,128)(2,1)S(1)}, bf16[16,2048,128]{2,1,0:T(8,128)(2,1)}, u32[]{:S(2)}) copy-start(bf16[16,2048,128]{2,1,0:T(8,128)(2,1)} %get-tuple-element.9) | copy-start | bytes 25165828
  414.6 4.3 %copy-start.2 = (bf16[16,512,128]{2,1,0:T(8,128)(2,1)S(1)}, bf16[16,512,128]{2,1,0:T(8,128)(2,1)}, u32[]{:S(2)}) copy-start(bf16[16,512,128]{2,1,0:T(8,128)(2,1)} %get-tuple-element.10) | copy-start | bytes 6291460
  414.6 5.6 %copy-start.1 = (bf16[16,512,128]{2,1,0:T(8,128)(2,1)S(1)}, bf16[16,512,128]{2,1,0:T(8,128)(2,1)}, u32[]{:S(2)}) copy-start(bf16[16,512,128]{2,1,0:T(8,128)(2,1)} %get-tuple-element.11) | copy-start | bytes 6291460

commit v3 on v2

--- a/solution.py
+++ b/solution.py
@@ -26,6 +26,7 @@
 NSLOT = 2
 NA = 10
 NP = NA // 2
+LAST = 2
 DIRECT = 5
 HOMES = (0, 0, 1, 2, 4, 5)
 HSLOT = (0, 1, 0, 0, 0, 0)
@@ -365,26 +366,26 @@
                     row_keep(p, j).wait()
                 for j in SENT.get(c, ()):
                     if c == 3 and j < 2:
-                        @pl.when(p < NP - 1)
+                        @pl.when(p < NP - LAST)
                         def _():
                             row_send(p, c, j).start()
 
-                        @pl.when(p == NP - 1)
+                        @pl.when(p >= NP - LAST)
                         def _():
-                            last_direct(j).start()
+                            last_direct(p, j).start()
                     else:
                         row_send(p, c, j).start()
                 if c == 1:
-                    @pl.when(p == NP - 1)
+                    @pl.when(p >= NP - LAST)
                     def _():
                         for j in range(2):
-                            last_onward(j).start()
-
-    def last_direct(j):
-        return remote(pp.at[NP - 1, j], lc.at[j], osend.at[NP - 1, j], lcr.at[j], plane(0))
-
-    def last_onward(j):
-        return remote(pp.at[NP - 1, j], la.at[NP - 1, j], osend.at[NP - 1, j], lar.at[NP - 1, j], plane(0))
+                            last_onward(p, j).start()
+
+    def last_direct(p, j):
+        return remote(pp.at[p, j], lc.at[p - (NP - LAST), j], osend.at[p, j], lcr.at[p - (NP - LAST), j], plane(0))
+
+    def last_onward(p, j):
+        return remote(pp.at[p, j], la.at[p, j], osend.at[p, j], lar.at[p, j], plane(0))
 
     def rows_left(p):
         for c, js in ((3, range(6)), (2, range(4))):
@@ -393,10 +394,10 @@
                 for j in js:
                     row_send(p, c, j).wait_send()
 
-        @pl.when((chip == 1) & (p == NP - 1))
+        @pl.when((chip == 1) & (p >= NP - LAST))
         def _():
             for j in range(2):
-                last_onward(j).wait_send()
+                last_onward(p, j).wait_send()
 
     def join_chip2(p):
         for j in (2, 3):
@@ -523,6 +524,11 @@
         def _():
             own_kv(task + 2, start)
 
+        for c in (2, 3):
+            @pl.when((chip == c) & (slot == 1) & (p + 1 < NP))
+            def _():
+                forward(p + 1, c)
+
         for when, rows in enumerate(LATER):
             @pl.when(task == when)
             def _():
@@ -548,14 +554,6 @@
             @pl.when((chip == 1) & (task + 1 < NP))
             def _():
                 forward(task + 1, 1)
-
-            @pl.when((chip == 2) & (slot == 1) & (p + 1 < NP))
-            def _():
-                forward(p + 1, 2)
-
-            @pl.when((chip == 3) & (task > 0) & (task < NP))
-            def _():
-                forward(task, 3)
 
             @pl.when(task + 1 < NA)
             def _():
@@ -804,11 +802,11 @@
             for j in range(2):
                 onward = lambda pq: remote(tmp(2 + j), la.at[pq, j], tout.at[j], lar.at[pq, j], plane(0))
 
-                @pl.when(p > 0)
+                @pl.when((p > 0) & (p <= NP - LAST))
                 def _():
                     onward(p - 1).wait_send()
 
-                @pl.when(p < NP - 1)
+                @pl.when(p < NP - LAST)
                 def _():
                     join(j)
                     tmp(2 + j)[...] = tmp(0)[...] + tmp(1)[...]
@@ -840,11 +838,12 @@
                 take(la.at[p, j], 1).wait()
                 take(lb.at[p, j], 2).wait()
 
-                @pl.when(p == NP - 1)
+                @pl.when(p >= NP - LAST)
                 def _():
-                    remote(lc.at[j], lc.at[j], fl.at[0, 0], lcr.at[j], other).wait_recv()
-                    take(lc.at[j], 3).start()
-                    take(lc.at[j], 3).wait()
+                    came_by = lc.at[p - (NP - LAST), j]
+                    remote(came_by, came_by, fl.at[0, 0], lcr.at[p - (NP - LAST), j], other).wait_recv()
+                    take(came_by, 3).start()
+                    take(came_by, 3).wait()
                     tmp(2)[...] += tmp(3)[...]
 
                 finish(p, j, tmp(0)[...] + tmp(1)[...] + tmp(2)[...])
@@ -921,7 +920,7 @@
                 shape((NA, NDEV), narrow), shape((NA, NDEV), narrow), shape((NP,), wide), shape((NP,), wide),
                 shape((2 * NDEV,), wide), shape((2 * NDEV,), wide),
                 shape((2, NDEV), narrow), shape((2, NDEV), narrow),
-                shape((NP, NDEV), pair, F32), shape((NP, 4), pair, F32), shape((NP, 2), pair, F32), shape((2,), pair, F32),
+                shape((NP, NDEV), pair, F32), shape((NP, 4), pair, F32), shape((NP, 2), pair, F32), shape((LAST, 2), pair, F32),
                 shape((NP, 6), pair, F32),
             ],
             in_specs=[any_spec] * 4,
@@ -938,7 +937,7 @@
                 vmem((HD, QR), BF16), vmem((HD, QR), BF16),
                 dma((2, NP, 4, 3)), dma((2, NP, NDEV)), dma((2, NP // 2)), dma((2, NP // 2)),
                 dma((4, len(HOMES))), dma((4, 2, NDEV)), dma((2, NSLOT)), dma((4, rows)), dma((4, NDEV)), dma((4, NSLOT)),
-                dma((NP, NDEV)), dma((NP, 4)), dma((NP, 2)), dma((2,)), dma((2, NDEV)), dma((NDEV,)), dma((2, 2)),
+                dma((NP, NDEV)), dma((NP, 4)), dma((NP, 2)), dma((LAST, 2)), dma((2, NDEV)), dma((NDEV,)), dma((2, 2)),
                 dma((4,)), dma((2,)), dma((NP, 6)), dma((2, 2 * NDEV)), dma((2, 2, NDEV)),
             ],
             compiler_params=pltpu.CompilerParams(

time: 423 us -> 412 us (0.974)
  the two profiles are of different devices: /device:TPU:2 before, /device:TPU:5 now
where the time goes in v3:
time: 412 us; the launch traced here: 411 us
  Pallas kernels  395 us (96%)
  local copies, waits for them, and re-layouts  16 us (4%)
    pallas_call x1, Pallas kernels, local_attn(): call(q_in.reshape((rows,) + wide), do_in.reshape((rows,) + wide), k_in.re...  395 us
    unnamed x10, local copies, waits for them, and re-layouts  16 us

profile of v3, /device:TPU:5, one launch (start us, length us, event | category | flops | bytes accessed | tf_op | source)
XLA Modules:
  0.0 411.2 jit_solution(7481740932214702500)
XLA Ops:
  0.6 394.6 %shard_map.75 = (bf16[16,2048,128]{2,1,0:T(8,128)(2,1)}, bf16[16,2048,128]{2,1,0:T(8,128)(2,1)}, bf16[16,512,128]{2,1,0:T(8,128)(2,1)}, bf16[16,512,128]{2,1,0:T...) custom-call(bf16[16,2048,128]{2,1,0:T(8,128)(2,1)} %bitcast.12, ...), custom_call_target="tpu_custom_call" | custom-call | tf_op jit(solution)/shard_map/pallas_call | solution.py:946
  395.2 0.0 copy-start
  395.2 9.1 %copy.14 = bf16[16,512,4,128]{3,2,1,0:T(4,128)(2,1)} copy(bf16[16,512,4,128]{3,2,1,0:T(4,128)(2,1)} %bitcast.15) | data formatting | bytes 16777216
  404.3 0.0 copy-done
  404.3 0.0 copy-start.2
  404.3 0.0 copy-start.1
  404.3 4.3 %copy.15 = bf16[16,512,4,128]{3,2,1,0:T(4,128)(2,1)} copy(bf16[16,512,4,128]{3,2,1,0:T(4,128)(2,1)S(1)} %bitcast.14) | data formatting | bytes 16777216
  408.6 0.0 copy-done.2
  408.6 1.3 copy.16
  409.9 0.0 copy-done.1
  409.9 1.3 copy.17
Async XLA Ops:
  395.2 9.1 %copy-start = (bf16[16,2048,128]{2,1,0:T(8,128)(2,1)S(1)}, bf16[16,2048,128]{2,1,0:T(8,128)(2,1)}, u32[]{:S(2)}) copy-start(bf16[16,2048,128]{2,1,0:T(8,128)(2,1)} %get-tuple-element.9) | copy-start | bytes 25165828
  404.3 4.3 %copy-start.2 = (bf16[16,512,128]{2,1,0:T(8,128)(2,1)S(1)}, bf16[16,512,128]{2,1,0:T(8,128)(2,1)}, u32[]{:S(2)}) copy-start(bf16[16,512,128]{2,1,0:T(8,128)(2,1)} %get-tuple-element.10) | copy-start | bytes 6291460
  404.3 5.6 %copy-start.1 = (bf16[16,512,128]{2,1,0:T(8,128)(2,1)S(1)}, bf16[16,512,128]{2,1,0:T(8,128)(2,1)}, u32[]{:S(2)}) copy-start(bf16[16,512,128]{2,1,0:T(8,128)(2,1)} %get-tuple-element.11) | copy-start | bytes 6291460

commit v4 on v3

--- a/solution.py
+++ b/solution.py
@@ -537,7 +537,7 @@
 
         fetch_wait(task)
 
-        @pl.when((slot == 0) & (p > 0))
+        @pl.when((slot == 0) & (p > 0) & (chip == 3))
         def _():
             rows_leave(p - 1)
 
@@ -566,6 +566,10 @@
                     @pl.loop(0, 2 * chip + 2)
                     def _(j):
                         pair_out(p - 1, j).wait_send()
+
+                    @pl.when(chip < 3)
+                    def _():
+                        rows_leave(p - 1)
 
                 acc[0] = jnp.zeros((2 * HD, SEQ), F32)
 
@@ -717,7 +721,7 @@
 
     def sum_down(t, h, j, away_too):
         target = sstage[t - 2].at[h, j] if away_too else rdst[t].at[home_row(h)]
-        return pltpu.make_async_copy(rbuf[t], target, lout.at[t, 0])
+        return pltpu.make_async_copy(rbuf[t].at[lax.rem(j, 2)], target, lout.at[t, lax.rem(j, 2)])
 
     def sum_away(t, h, j):
         row = home_row(h)
@@ -760,29 +764,48 @@
         put_down_start(1, task)
         send_away(0, task)
 
-        def flush(j):
+        def convert(j):
             o = pl.ds(pl.multiple_of(j * BLK, BLK), BLK)
-            kst[...] = (acc[h, pl.ds(0, HD), o] * SCALE).T.astype(BF16)
-            vst[...] = acc[h, pl.ds(HD, HD), o].T.astype(BF16)
-            for where, away_too in ((j == me, False), (j != me, True)):
-                @pl.when(where)
-                def _():
-                    for t in (2, 3):
-                        sum_down(t, h, j, away_too).start()
-                    for t in (2, 3):
-                        sum_down(t, h, j, away_too).wait()
-                        if away_too:
-                            sum_away(t, h, j).start()
+            kst[lax.rem(j, 2)] = (acc[h, pl.ds(0, HD), o] * SCALE).T.astype(BF16)
+            vst[lax.rem(j, 2)] = acc[h, pl.ds(HD, HD), o].T.astype(BF16)
+
+        def down(j, away_too, what):
+            for t in (2, 3):
+                what(sum_down(t, h, j, away_too))
+
+        def leave(j):
+            down(j, True, lambda cp: cp.wait())
+            for t in (2, 3):
+                sum_away(t, h, j).start()
 
         @pl.when(step >= 2 * chip)
         def _():
-            flush(i)
+            convert(i)
+
+            @pl.when(i == me)
+            def _():
+                down(i, False, start)
+                down(i, False, lambda cp: cp.wait())
+
+            @pl.when(i != me)
+            def _():
+                down(i, True, start)
+                leave(i)
 
         @pl.when(step == NDEV - 1)
         def _():
             @pl.loop(0, 2 * chip)
             def _(j):
-                flush(j)
+                convert(j)
+                down(j, True, start)
+
+                @pl.when(j > 0)
+                def _():
+                    leave(j - 1)
+
+            @pl.when(chip > 0)
+            def _():
+                leave(2 * chip - 1)
 
     @pl.when(hcount > 0)
     def _():
@@ -878,7 +901,7 @@
         home_out(hi, finished)
 
     def came(t, row):
-        source = rbuf[t].at[0] if t < 2 else rbuf[t]
+        source = rbuf[t].at[0]
         remote(source, rdst[t].at[row], rsend.at[t, 0], rrecv.at[t, row], other).wait_recv()
 
     for hi in range(len(HOMES)):
@@ -929,7 +952,7 @@
                 vmem((2,) + wide, BF16), vmem((2,) + wide, BF16),
                 vmem((2, SEQ, HD), BF16), vmem((2, SEQ, HD), BF16),
                 vmem((NSLOT,) + wide, BF16), vmem((NSLOT,) + wide, BF16),
-                vmem((BLK, HD), BF16), vmem((BLK, HD), BF16),
+                vmem((2, BLK, HD), BF16), vmem((2, BLK, HD), BF16),
                 vmem((2, 2) + narrow, BF16),
                 vmem((QR, SEQ), F32), vmem((2, 2 * HD, SEQ), F32),
                 vmem((QR, HD), F32),

time: 412 us -> 410 us (level)
  the two profiles are of different devices: /device:TPU:5 before, /device:TPU:1 now
where the time goes in v4:
time: 410 us; the launch traced here: 409 us
  Pallas kernels  392 us (96%)
  local copies, waits for them, and re-layouts  16 us (4%)
    pallas_call x1, Pallas kernels, local_attn(): call(q_in.reshape((rows,) + wide), do_in.reshape((rows,) + wide), k_in.re...  392 us
    unnamed x10, local copies, waits for them, and re-layouts  16 us

profile of v4, /device:TPU:1, one launch (start us, length us, event | category | flops | bytes accessed | tf_op | source)
XLA Modules:
  0.0 408.9 jit_solution(12948184976125398493)
XLA Ops:
  0.6 392.3 %shard_map.75 = (bf16[16,2048,128]{2,1,0:T(8,128)(2,1)}, bf16[16,2048,128]{2,1,0:T(8,128)(2,1)}, bf16[16,512,128]{2,1,0:T(8,128)(2,1)}, bf16[16,512,128]{2,1,0:T...) custom-call(bf16[16,2048,128]{2,1,0:T(8,128)(2,1)} %bitcast.12, ...), custom_call_target="tpu_custom_call" | custom-call | tf_op jit(solution)/shard_map/pallas_call | solution.py:969
  392.9 0.0 copy-start
  392.9 9.1 %copy.14 = bf16[16,512,4,128]{3,2,1,0:T(4,128)(2,1)} copy(bf16[16,512,4,128]{3,2,1,0:T(4,128)(2,1)} %bitcast.15) | data formatting | bytes 16777216
  402.0 0.0 copy-done
  402.0 0.0 copy-start.2
  402.0 0.0 copy-start.1
  402.0 4.3 %copy.15 = bf16[16,512,4,128]{3,2,1,0:T(4,128)(2,1)} copy(bf16[16,512,4,128]{3,2,1,0:T(4,128)(2,1)S(1)} %bitcast.14) | data formatting | bytes 16777216
  406.2 0.0 copy-done.2
  406.2 1.3 copy.16
  407.6 0.0 copy-done.1
  407.6 1.3 copy.17
Async XLA Ops:
  392.9 9.1 %copy-start = (bf16[16,2048,128]{2,1,0:T(8,128)(2,1)S(1)}, bf16[16,2048,128]{2,1,0:T(8,128)(2,1)}, u32[]{:S(2)}) copy-start(bf16[16,2048,128]{2,1,0:T(8,128)(2,1)} %get-tuple-element.9) | copy-start | bytes 25165828
  402.0 4.3 %copy-start.2 = (bf16[16,512,128]{2,1,0:T(8,128)(2,1)S(1)}, bf16[16,512,128]{2,1,0:T(8,128)(2,1)}, u32[]{:S(2)}) copy-start(bf16[16,512,128]{2,1,0:T(8,128)(2,1)} %get-tuple-element.10) | copy-start | bytes 6291460
  402.0 5.6 %copy-start.1 = (bf16[16,512,128]{2,1,0:T(8,128)(2,1)S(1)}, bf16[16,512,128]{2,1,0:T(8,128)(2,1)}, u32[]{:S(2)}) copy-start(bf16[16,512,128]{2,1,0:T(8,128)(2,1)} %get-tuple-element.11) | copy-start | bytes 6291460

commit v5 on v4

--- a/solution.py
+++ b/solution.py
@@ -26,7 +26,7 @@
 NSLOT = 2
 NA = 10
 NP = NA // 2
-LAST = 2
+LAST = 1
 DIRECT = 5
 HOMES = (0, 0, 1, 2, 4, 5)
 HSLOT = (0, 1, 0, 0, 0, 0)

time: 410 us -> 409 us (level)
  the two profiles are of different devices: /device:TPU:1 before, /device:TPU:2 now
where the time goes in v5:
time: 409 us; the launch traced here: 408 us
  Pallas kernels  391 us (96%)
  local copies, waits for them, and re-layouts  16 us (4%)
    pallas_call x1, Pallas kernels, local_attn(): call(q_in.reshape((rows,) + wide), do_in.reshape((rows,) + wide), k_in.re...  391 us
    unnamed x10, local copies, waits for them, and re-layouts  16 us

profile of v5, /device:TPU:2, one launch (start us, length us, event | category | flops | bytes accessed | tf_op | source)
XLA Modules:
  0.0 408.1 jit_solution(9538802559019443136)
XLA Ops:
  0.6 391.5 %shard_map.75 = (bf16[16,2048,128]{2,1,0:T(8,128)(2,1)}, bf16[16,2048,128]{2,1,0:T(8,128)(2,1)}, bf16[16,512,128]{2,1,0:T(8,128)(2,1)}, bf16[16,512,128]{2,1,0:T...) custom-call(bf16[16,2048,128]{2,1,0:T(8,128)(2,1)} %bitcast.12, ...), custom_call_target="tpu_custom_call" | custom-call | tf_op jit(solution)/shard_map/pallas_call | solution.py:969
  392.1 0.0 copy-start
  392.1 9.1 %copy.14 = bf16[16,512,4,128]{3,2,1,0:T(4,128)(2,1)} copy(bf16[16,512,4,128]{3,2,1,0:T(4,128)(2,1)} %bitcast.15) | data formatting | bytes 16777216
  401.2 0.0 copy-done
  401.2 0.0 copy-start.2
  401.2 0.0 copy-start.1
  401.2 4.3 %copy.15 = bf16[16,512,4,128]{3,2,1,0:T(4,128)(2,1)} copy(bf16[16,512,4,128]{3,2,1,0:T(4,128)(2,1)S(1)} %bitcast.14) | data formatting | bytes 16777216
  405.5 0.0 copy-done.2
  405.5 1.3 copy.16
  406.8 0.0 copy-done.1
  406.8 1.3 copy.17
Async XLA Ops:
  392.1 9.1 %copy-start = (bf16[16,2048,128]{2,1,0:T(8,128)(2,1)S(1)}, bf16[16,2048,128]{2,1,0:T(8,128)(2,1)}, u32[]{:S(2)}) copy-start(bf16[16,2048,128]{2,1,0:T(8,128)(2,1)} %get-tuple-element.9) | copy-start | bytes 25165828
  401.2 4.3 %copy-start.2 = (bf16[16,512,128]{2,1,0:T(8,128)(2,1)S(1)}, bf16[16,512,128]{2,1,0:T(8,128)(2,1)}, u32[]{:S(2)}) copy-start(bf16[16,512,128]{2,1,0:T(8,128)(2,1)} %get-tuple-element.10) | copy-start | bytes 6291460
  401.2 5.6 %copy-start.1 = (bf16[16,512,128]{2,1,0:T(8,128)(2,1)S(1)}, bf16[16,512,128]{2,1,0:T(8,128)(2,1)}, u32[]{:S(2)}) copy-start(bf16[16,512,128]{2,1,0:T(8,128)(2,1)} %get-tuple-element.11) | copy-start | bytes 6291460
